TPU v7x, 32 devices: a whole 2x2x4 slice. The times are simulated.
32 devices in a mesh: gx: 4 (over y, core), gy: 2 (over x), gz: 4 (over z).
Axes of the slice: x: 2, y: 2, z: 4, core: 2. Of those that a mesh axis runs over, the one named last changes fastest.
Arguments:
- node_latent: bfloat16 [64, 64, 16, 128], P('gx', 'gy', 'gz'), may hold values from -6 to 6
- edge_latent: bfloat16 [4, 2, 4, 12288, 128], P('gx', 'gy', 'gz'), may hold values from -6 to 6
- senders: int32 [4, 2, 4, 12288], P('gx', 'gy', 'gz'), may hold values from 7 to 3664, as said below
- receivers: int32 [4, 2, 4, 12288], P('gx', 'gy', 'gz'), may hold values from 0 to 2047, as said below
- w1_edge: bfloat16 [384, 128], replicated, may hold values from -0.3125 to 0.3125
- b1_edge: float32 [128], replicated, may hold values from -3 to 3
- w2_edge: bfloat16 [128, 128], replicated, may hold values from -0.5 to 0.5
- b2_edge: float32 [128], replicated, may hold values from -3 to 3
- w1_node: bfloat16 [256, 128], replicated, may hold values from -0.375 to 0.375
- b1_node: float32 [128], replicated, may hold values from -3 to 3
- w2_node: bfloat16 [128, 128], replicated, may hold values from -0.5 to 0.5
- cot_node: bfloat16 [64, 64, 16, 128], P('gx', 'gy', 'gz'), may hold values from -6 to 6
- cot_edge: bfloat16 [4, 2, 4, 12288, 128], P('gx', 'gy', 'gz'), may hold values from -8 to 8
Outputs:
- grad_node: bfloat16 [64, 64, 16, 128], P('gx', 'gy', 'gz')
- grad_edge: bfloat16 [4, 2, 4, 12288, 128], P('gx', 'gy', 'gz')
- grad_w1_edge: float32 [384, 128], replicated
- grad_w2_edge: float32 [128, 128], replicated
- grad_w1_node: float32 [256, 128], replicated
- grad_w2_node: float32 [128, 128], replicated
- grad_biases: float32 [4, 128], replicated
Inputs may be any that keep to these rules, and one draw needn't show every extreme that they name: `receivers`: in every block the list is nondecreasing; entry (i * 32 + j) * 4 + l names the block's cell at local coordinates (i, j, l). `senders`: entry (p * 34 + q) * 6 + r names the cell at local coordinates (p - 1, q - 1, r - 1) of the block extended by one cell on every side, the extension being cells of the adjacent blocks around the periodic box; it is always one of the six face neighbours of the same slot's receiver.
All inputs are finite; a program needn't handle non-finite values.
Results may differ from a plain program's by a relative error of at most 0.01.
Values may be sent and summed in bfloat16 or wider, within the bound.
A program may use at most 128 MiB of HBM per device.

v0:
```python
import jax
import jax.numpy as jnp
from jax import lax
from jax.sharding import PartitionSpec as P


def padded_2(cells, sides, width):
    for axis, dim in sides:
        count = lax.axis_size(axis)
        head = lax.slice_in_dim(cells, 0, width, axis=dim)
        tail = lax.slice_in_dim(cells, cells.shape[dim] - width, cells.shape[dim], axis=dim)
        cells = jnp.concatenate(
            [
                lax.ppermute(tail, axis, [(i, (i + 1) % count) for i in range(count)]),
                cells,
                lax.ppermute(head, axis, [((i + 1) % count, i) for i in range(count)]),
            ],
            axis=dim,
        )
    return cells


def transposed_dot(left, right):
    return lax.dot_general(
        left, right, (((0,), (0,)), ((), ())), preferred_element_type=jnp.float32
    )


def column_sums(values):
    return jnp.sum(values.astype(jnp.float32), axis=0)


def silu_slope(values):
    sigma = jax.nn.sigmoid(values)
    return sigma * (1.0 + values * (1.0 - sigma))


def reduce_flat(flat_grads):
    return lax.psum(flat_grads, ("gx", "gy", "gz"))


def on_device(
    node_latent,
    edge_latent,
    senders,
    receivers,
    w1_edge,
    b1_edge,
    w2_edge,
    b2_edge,
    w1_node,
    b1_node,
    w2_node,
    cot_node,
    cot_edge,
):
    side_x, side_y, side_z, latent = node_latent.shape
    cell_count = side_x * side_y * side_z
    edge_count = edge_latent.shape[3]
    padded = padded_2(node_latent, (("gx", 0), ("gy", 1), ("gz", 2)), 1)
    flat_pad = padded.reshape(-1, latent)
    own_rows = node_latent.reshape(cell_count, latent)
    edge_rows = edge_latent.reshape(edge_count, latent)
    cot_rows = cot_edge.reshape(edge_count, latent)
    cot_cells = cot_node.reshape(cell_count, latent)
    sender_ids = senders.reshape(edge_count)
    receiver_ids = receivers.reshape(edge_count)
    sender_rows = jnp.take(flat_pad, sender_ids, axis=0)
    receiver_rows = jnp.take(own_rows, receiver_ids, axis=0)
    x_edge = jnp.concatenate([edge_rows, sender_rows, receiver_rows], axis=1)
    z_edge = jnp.dot(x_edge, w1_edge, preferred_element_type=jnp.float32) + b1_edge
    u_edge = jax.nn.silu(z_edge).astype(jnp.bfloat16)
    edge_new = (
        edge_rows.astype(jnp.float32)
        + jnp.dot(u_edge, w2_edge, preferred_element_type=jnp.float32)
        + b2_edge
    ).astype(jnp.bfloat16)
    aggregate = jax.ops.segment_sum(
        edge_new.astype(jnp.float32), receiver_ids, cell_count, indices_are_sorted=True
    ).astype(jnp.bfloat16)
    x_node = jnp.concatenate([own_rows, aggregate], axis=1)
    z_node = jnp.dot(x_node, w1_node, preferred_element_type=jnp.float32) + b1_node
    u_node = jax.nn.silu(z_node).astype(jnp.bfloat16)
    dz_node = (
        jnp.dot(cot_cells, w2_node.T, preferred_element_type=jnp.float32) * silu_slope(z_node)
    ).astype(jnp.bfloat16)
    dx_node = jnp.dot(dz_node, w1_node.T, preferred_element_type=jnp.float32)
    node_flat = jnp.concatenate(
        [
            transposed_dot(x_node, dz_node).reshape(-1),
            column_sums(dz_node),
            transposed_dot(u_node, cot_cells).reshape(-1),
            column_sums(cot_cells),
        ]
    )
    d_edge = (
        cot_rows.astype(jnp.float32) + jnp.take(dx_node[:, latent:], receiver_ids, axis=0)
    ).astype(jnp.bfloat16)
    dz_edge = (
        jnp.dot(d_edge, w2_edge.T, preferred_element_type=jnp.float32) * silu_slope(z_edge)
    ).astype(jnp.bfloat16)
    d_self = jnp.dot(dz_edge, w1_edge[:latent].T, preferred_element_type=jnp.float32)
    d_sender = jnp.dot(dz_edge, w1_edge[latent : 2 * latent].T, preferred_element_type=jnp.float32)
    d_receiver = jnp.dot(dz_edge, w1_edge[2 * latent :].T, preferred_element_type=jnp.float32)
    grad_edge = (
        (d_edge.astype(jnp.float32) + d_self).astype(jnp.bfloat16).reshape(edge_latent.shape)
    )
    edge_flat = jnp.concatenate(
        [
            transposed_dot(x_edge, dz_edge).reshape(-1),
            column_sums(dz_edge),
            transposed_dot(u_edge, d_edge).reshape(-1),
            column_sums(d_edge),
        ]
    )
    summed = (reduce_flat(jnp.concatenate([node_flat, edge_flat])),)
    send_grid = jax.ops.segment_sum(d_sender, sender_ids, flat_pad.shape[0]).reshape(
        side_x + 2, side_y + 2, side_z + 2, latent
    )
    receiver_sum = jax.ops.segment_sum(
        d_receiver, receiver_ids, cell_count, indices_are_sorted=True
    )
    own_terms = cot_cells.astype(jnp.float32) + dx_node[:, :latent] + receiver_sum
    interior = send_grid[1:-1, 1:-1, 1:-1] + own_terms.reshape(side_x, side_y, side_z, latent)
    pair_x = jnp.stack([send_grid[0, 1:-1, 1:-1], send_grid[-1, 1:-1, 1:-1]], axis=0)
    back_x = padded_2(pair_x.astype(jnp.bfloat16), (("gx", 0),), 1).astype(pair_x.dtype)
    interior = interior.at[0].add(back_x[0]).at[-1].add(back_x[3])
    pair_y = jnp.stack([send_grid[1:-1, 0, 1:-1], send_grid[1:-1, -1, 1:-1]], axis=1)
    back_y = padded_2(pair_y.astype(jnp.bfloat16), (("gy", 1),), 1).astype(pair_y.dtype)
    interior = interior.at[:, 0].add(back_y[:, 0]).at[:, -1].add(back_y[:, 3])
    pair_z = jnp.stack([send_grid[1:-1, 1:-1, 0], send_grid[1:-1, 1:-1, -1]], axis=2)
    back_z = padded_2(pair_z.astype(jnp.bfloat16), (("gz", 2),), 1).astype(pair_z.dtype)
    interior = interior.at[:, :, 0].add(back_z[:, :, 0]).at[:, :, -1].add(back_z[:, :, 3])
    grad_node = interior.astype(jnp.bfloat16)
    param_count = 7 * latent * latent + 4 * latent
    partial_value = sum((jnp.sum(portion * portion) for portion in summed))
    factor = 1.0 / jnp.maximum(1.0, jnp.sqrt(partial_value / param_count))
    scaled = [portion * factor for portion in summed]
    full_grads = scaled[0]
    square = latent * latent
    cut_a = 2 * square
    cut_b = cut_a + latent
    cut_c = cut_b + square
    cut_d = cut_c + latent
    cut_e = cut_d + 3 * square
    cut_f = cut_e + latent
    cut_g = cut_f + square
    grad_w1_node = full_grads[:cut_a].reshape(2 * latent, latent)
    bias_one_node = full_grads[cut_a:cut_b]
    grad_w2_node = full_grads[cut_b:cut_c].reshape(latent, latent)
    bias_two_node = full_grads[cut_c:cut_d]
    grad_w1_edge = full_grads[cut_d:cut_e].reshape(3 * latent, latent)
    bias_one_edge = full_grads[cut_e:cut_f]
    grad_w2_edge = full_grads[cut_f:cut_g].reshape(latent, latent)
    bias_two_edge = full_grads[cut_g:]
    grad_biases = jnp.stack([bias_one_edge, bias_two_edge, bias_one_node, bias_two_node])
    return (
        grad_node,
        grad_edge,
        grad_w1_edge,
        grad_w2_edge,
        grad_w1_node,
        grad_w2_node,
        grad_biases,
    )


def solution(mesh):
    placed = (
        P("gx", "gy", "gz", None),
        P("gx", "gy", "gz", None, None),
        P("gx", "gy", "gz", None),
        P("gx", "gy", "gz", None),
        P(),
        P(),
        P(),
        P(),
        P(),
        P(),
        P(),
        P("gx", "gy", "gz", None),
        P("gx", "gy", "gz", None, None),
    )
    return jax.shard_map(
        on_device,
        mesh=mesh,
        in_specs=placed,
        out_specs=(
            P("gx", "gy", "gz", None),
            P("gx", "gy", "gz", None, None),
            P(),
            P(),
            P(),
            P(),
            P(),
        ),
        check_vma=False,
    )
```

profile of v0, /device:TPU:0, one launch (start us, length us, event | category | flops | bytes accessed | tf_op | source)
XLA Modules:
  0.0 507.3 jit_solution(1856447125221227902)
XLA Ops:
  24.9 43.6 %gather_fusion.1 = bf16[12288,128]{1,0:T(8,128)(2,1)} fusion(bf16[2048,128]{1,0:T(8,128)(2,1)S(1)} %bitcast.62, s32[12288]{0:T(1024)S(1)} %broadcast_clamp_fusion), kind=kCustom, calls=%fused_computation.1 | custom fusion | bytes 6340608 | tf_op jit(solution)/shard_map/jit(_take)/gather | solution.py:69
  70.1 43.7 %gather_fusion = bf16[12288,128]{1,0:T(8,128)(2,1)} fusion(bf16[3672,128]{1,0:T(8,128)(2,1)S(1)} %reshape.366, s32[12288]{0:T(1024)S(1)} %broadcast_clamp_fusion.1), kind=kCustom, calls=%fused_computation | custom fusion | bytes 6340608 | tf_op jit(solution)/shard_map/jit(_take)/gather | solution.py:68
  113.8 9.2 %broadcast_select_fusion = (bf16[12288,128]{1,0:T(8,128)(2,1)S(1)}, bf16[12288,128]{1,0:T(8,128)(2,1)S(1)}) fusion(bf16[12288,128]{1,0:T(8,128)(2,1)} %gather_fusion, pred[12288]{0:T(1024)(128)(4,1)S(1)} %compare_and_fusion, bf16[12288,128]{1,0:T(8,128)(2,1)} %gather_fusion.1, pred[12288]{0:T(1024)(128)(4,1)S(1)} %compare_and_fusion.1), kind=kLoop, calls=%fused_computation.26 | loop fusion | flops 3145728 | bytes 12607488 | tf_op jit(solution)/shard_map/jit(_take)/select_n | solution.py:68
  123.1 3.0 convolution_add_fusion.2
  126.1 2.6 copy-done.22
  128.8 3.8 fusion.4
  132.6 76.0 %scatter_custom_fusion = f32[2048,128]{1,0:T(8,128)S(1)} fusion(s32[12288]{0:T(1024)S(1)} %bitcast.69, f32[12288,128]{1,0:T(8,128)} %fusion.4, f32[]{:T(128)} %constant.205.clone.1), kind=kCustom, calls=%fused_computation.43 | custom fusion | flops 1572864 | bytes 1049088 | tf_op jit(solution)/shard_map/scatter-add | solution.py:78
  211.8 41.5 %gather_fusion.2 = f32[12288,128]{1,0:T(8,128)} fusion(f32[2048,128]{1,0:T(8,128)S(1)} %get-tuple-element.81, s32[12288]{0:T(1024)S(1)} %broadcast_clamp_fusion), kind=kCustom, calls=%fused_computation.2 | custom fusion | bytes 12632064 | tf_op jit(solution)/shard_map/jit(_take)/gather | solution.py:97
  253.4 9.3 %convert_reduce_fusion = (f32[128]{0:T(128)S(1)}, bf16[12288,128]{1,0:T(8,128)(2,1)S(1)}) fusion(f32[12288,128]{1,0:T(8,128)} %gather_fusion.2, pred[12288]{0:T(1024)(128)(4,1)S(1)} %compare_and_fusion.1, bf16[1,1,1,12288,128]{4,3,2,1,0:T(8,128)(2,1)} %param.37), kind=kLoop, calls=%fused_computation.17 | loop fusion | flops 9437056 | bytes 12595712 | tf_op jit(solution)/shard_map/reduce_sum | solution.py:30
  262.7 5.4 %convolution_bitcast_fusion.2 = f32[16384]{0:T(1024)} fusion(bf16[12288,128]{1,0:T(8,128)(2,1)S(1)} %get-tuple-element.80, f32[12288,128]{1,0:T(8,128)} %copy-done.22), kind=kOutput, calls=%fused_computation.31 | convolution fusion | flops 410517504 | bytes 9502720 | tf_op jit(solution)/shard_map/dot_general | solution.py:24
  268.2 2.7 convert_reduce_fusion.1
  271.9 3.3 convolution_bitcast_fusion
  275.2 2.6 fusion.5
  277.9 3.6 fusion.20
  281.5 3.6 fusion.22
  285.1 66.6 %scatter_custom_fusion.1 = f32[3672,128]{1,0:T(8,128)S(1)} fusion(s32[12288]{0:T(1024)} %bitcast.74, f32[12288,128]{1,0:T(8,128)} %fusion.22, f32[]{:T(128)} %constant.205.clone.1), kind=kCustom, calls=%fused_computation.41 | custom fusion | flops 1572864 | bytes 1880576 | tf_op jit(solution)/shard_map/scatter-add | solution.py:117
  366.7 76.2 %scatter_fusion = f32[2048,128]{1,0:T(8,128)S(1)} fusion(f32[2048,128]{1,0:T(8,128)S(1)} %get-tuple-element.82, s32[12288]{0:T(1024)S(1)} %bitcast.70, f32[12288,128]{1,0:T(8,128)} %fusion.20), kind=kCustom, calls=%fused_computation.5 | custom fusion | flops 1572864 | bytes 18923520 | tf_op jit(solution)/shard_map/scatter-add | solution.py:120
  448.9 3.8 collective-permute-start.11
  452.9 7.2 %collective-permute-done.10 = bf16[16,32,1,128]{3,2,1,0:T(2,128)(2,1)S(1)} collective-permute-done((bf16[16,32,1,128]{3,2,1,0:T(2,128)(2,1)S(1)}, bf16[16,32,1,128]{3,2,1,0:T(2,128)(2,1)S(1)}, u32[]{:S(2)}, u32[]{:S(2)}) %collective-permute-start.10) | collective-permute-done | bytes 131104 | tf_op jit(solution)/shard_map/ppermute | solution.py:14
  460.0 2.5 collective-permute-done.11
  463.8 5.3 %scatter-add.58 = f32[16,32,4,128]{3,2,1,0:T(4,128)S(1)} dynamic-update-slice(f32[16,32,4,128]{3,2,1,0:T(4,128)S(1)} %fusion.17, f32[16,32,1,128]{3,2,1,0:T(1,128)S(1)} %convert_add_fusion.1, s32[]{:T(128)} %constant.206.clone.1, s32[]{:T(128)} %constant.206.clone.1, s32[]{:T(128)} %constant.206.clone.1, s32[]{:T(128)} %constant.206.clone.1) | dynamic-update-slice | bytes 524292 | tf_op jit(solution)/shard_map/scatter-add | solution.py:133
  469.1 2.4 fusion.14
  471.5 5.3 %scatter-add.59 = f32[16,32,4,128]{3,2,1,0:T(4,128)S(1)} dynamic-update-slice(f32[16,32,4,128]{3,2,1,0:T(4,128)S(1)} %scatter-add.58, f32[16,32,1,128]{3,2,1,0:T(1,128)S(1)} %fusion.14, s32[]{:T(128)} %constant.206.clone.1, s32[]{:T(128)} %constant.206.clone.1, s32[]{:T(128)} %constant.216.clone.1, s32[]{:T(128)} %constant.206.clone.1) | dynamic-update-slice | bytes 524292 | tf_op jit(solution)/shard_map/scatter-add | solution.py:133
  477.8 16.5 %all-reduce.2.cloned.1.call-done = f32[115200]{0:T(1024)} async-done(((f32[115200]{0:T(1024)}), f32[115200]{0:T(1024)}) %all-reduce.2.cloned.1.call-update) | async-done | bytes 460816 | tf_op jit(solution)/shard_map/psum | solution.py:39
  (124 shorter events, 52.2 us)
Async XLA Ops:
  7.2 201.5 %copy-start = (bf16[256,128]{1,0:T(8,128)(2,1)S(1)}, bf16[256,128]{1,0:T(8,128)(2,1)}, u32[]{:S(2)}) copy-start(bf16[256,128]{1,0:T(8,128)(2,1)} %param.33) | copy-start | bytes 196612
  7.2 17.7 %copy-start.2 = (bf16[16,32,4,128]{3,2,1,0:T(4,128)(2,1)S(1)}, bf16[16,32,4,128]{3,2,1,0:T(4,128)(2,1)}, u32[]{:S(2)}) copy-start(bf16[16,32,4,128]{3,2,1,0:T(4,128)(2,1)} %param.25) | copy-start | bytes 1572868
  7.2 487.1 %all-reduce.2.cloned.1.call-start = ((), (), s32[]{:S(2)}) async-start(), calls=%async_computation | async-start | bytes 925696 | tf_op jit(solution)/shard_map/psum | solution.py:39
  8.1 4.3 collective-permute-start
  8.7 5.0 collective-permute-start.1
  13.8 4.4 collective-permute-start.2
  16.0 4.0 collective-permute-start.3
  20.2 48.9 %collective-permute-start.4 = (bf16[18,34,1,128]{3,1,2,0:T(8,128)(2,1)S(1)}, bf16[18,34,1,128]{3,1,2,0:T(8,128)(2,1)S(1)}, u32[]{:S(2)}, u32[]{:S(2)}) collective-permute-start(bf16[18,34,1,128]{3,1,2,0:T(8,128)(2,1)S(1)} %get-tuple-element.89), channel_id=1, source_target_pairs={{0,1},{1,2},{2,3},{3,0},{4,5},{5,6},{6,7},{7,4},{8,9},{9,10},{10,1... | collective-permute-start | bytes 470024 | tf_op jit(solution)/shard_map/ppermute | solution.py:14
  21.8 47.3 %collective-permute-start.5 = (bf16[18,34,1,128]{3,1,2,0:T(8,128)(2,1)S(1)}, bf16[18,34,1,128]{3,1,2,0:T(8,128)(2,1)S(1)}, u32[]{:S(2)}, u32[]{:S(2)}) collective-permute-start(bf16[18,34,1,128]{3,1,2,0:T(8,128)(2,1)S(1)} %get-tuple-element.90), channel_id=1, source_target_pairs={{1,0},{2,1},{3,2},{0,3},{5,4},{6,5},{7,6},{4,7},{9,8},{10,9},{11,1... | collective-permute-start | bytes 470024 | tf_op jit(solution)/shard_map/ppermute | solution.py:16
  24.9 43.6 %copy-start.9 = (bf16[16,32,4,128]{3,2,1,0:T(4,128)(2,1)S(1)}, bf16[16,32,4,128]{3,2,1,0:T(4,128)(2,1)}, u32[]{:S(2)}) copy-start(bf16[16,32,4,128]{3,2,1,0:T(4,128)(2,1)} %param.36) | copy-start | bytes 1572868
  113.8 9.3 %copy-start.12 = (bf16[384,128]{1,0:T(8,128)(2,1)S(1)}, bf16[384,128]{1,0:T(8,128)(2,1)}, u32[]{:S(2)}) copy-start(bf16[384,128]{1,0:T(8,128)(2,1)} %param.29) | copy-start | bytes 294916
  113.8 9.3 %copy-start.14 = (bf16[1,1,1,12288,128]{4,3,2,1,0:T(8,128)(2,1)S(1)}, bf16[1,1,1,12288,128]{4,3,2,1,0:T(8,128)(2,1)}, u32[]{:S(2)}) copy-start(bf16[1,1,1,12288,128]{4,3,2,1,0:T(8,128)(2,1)} %param.26) | copy-start | bytes 9437188
  113.8 9.3 %copy-start.19 = (f32[128]{0:T(128)S(1)}, f32[128]{0:T(128)}, u32[]{:S(2)}) copy-start(f32[128]{0:T(128)} %param.30) | copy-start | bytes 1540
  128.8 79.9 %copy-start.21 = (f32[128]{0:T(128)S(1)}, f32[128]{0:T(128)}, u32[]{:S(2)}) copy-start(f32[128]{0:T(128)} %param.34) | copy-start | bytes 1540
  253.4 14.8 %slice-start = ((s8[6291456]{0:T(1024)(128)(4,1)}), s8[4194304]{0:T(1024)(128)(4,1)S(1)}, s32[]{:S(2)}) async-start(s8[6291456]{0:T(1024)(128)(4,1)} %bitcast.77), calls=%async_computation.1 | async-start | bytes 8388608
  353.5 7.5 %copy-start.11 = (f32[49152]{0:T(1024)S(1)}, f32[49152]{0:T(1024)}, u32[]{:S(2)}) copy-start(f32[49152]{0:T(1024)} %convolution_bitcast_fusion) | copy-start | bytes 589828
  353.5 10.4 %copy-start.13 = (f32[16384]{0:T(1024)S(1)}, f32[16384]{0:T(1024)}, u32[]{:S(2)}) copy-start(f32[16384]{0:T(1024)} %convolution_bitcast_fusion.2) | copy-start | bytes 196612
  444.9 3.9 collective-permute-start.6
  445.0 7.7 %collective-permute-start.7 = (bf16[1,32,4,128]{3,2,1,0:T(4,128)(2,1)S(1)}, bf16[1,32,4,128]{3,2,1,0:T(4,128)(2,1)S(1)}, u32[]{:S(2)}, u32[]{:S(2)}) collective-permute-start(bf16[1,32,4,128]{3,2,1,0:T(4,128)(2,1)S(1)} %get-tuple-element.88), channel_id=1, source_target_pairs={{8,0},{16,8},{24,16},{0,24},{9,1},{17,9},{25,17},{1,25},{10,2},{18... | collective-permute-start | bytes 98312 | tf_op jit(solution)/shard_map/ppermute | solution.py:16
  446.7 6.1 %collective-permute-start.8 = (bf16[16,1,4,128]{3,2,1,0:T(4,128)(2,1)S(1)}, bf16[16,1,4,128]{3,2,1,0:T(4,128)(2,1)S(1)}, u32[]{:S(2)}, u32[]{:S(2)}) collective-permute-start(bf16[16,1,4,128]{3,2,1,0:T(4,128)(2,1)S(1)} %get-tuple-element.85), channel_id=1, source_target_pairs={{0,4},{4,0},{1,5},{5,1},{2,6},{6,2},{3,7},{7,3},{8,12},{12,8},{9,1... | collective-permute-start | bytes 49160 | tf_op jit(solution)/shard_map/ppermute | solution.py:14
  447.3 5.5 %collective-permute-start.9 = (bf16[16,1,4,128]{3,2,1,0:T(4,128)(2,1)S(1)}, bf16[16,1,4,128]{3,2,1,0:T(4,128)(2,1)S(1)}, u32[]{:S(2)}, u32[]{:S(2)}) collective-permute-start(bf16[16,1,4,128]{3,2,1,0:T(4,128)(2,1)S(1)} %get-tuple-element.86), channel_id=1, source_target_pairs={{4,0},{0,4},{5,1},{1,5},{6,2},{2,6},{7,3},{3,7},{12,8},{8,12},{13,... | collective-permute-start | bytes 49160 | tf_op jit(solution)/shard_map/ppermute | solution.py:16
  448.8 11.2 %collective-permute-start.10 = (bf16[16,32,1,128]{3,2,1,0:T(2,128)(2,1)S(1)}, bf16[16,32,1,128]{3,2,1,0:T(2,128)(2,1)S(1)}, u32[]{:S(2)}, u32[]{:S(2)}) collective-permute-start(bf16[16,32,1,128]{3,2,1,0:T(2,128)(2,1)S(1)} %copy-done.7), channel_id=1, source_target_pairs={{0,1},{1,2},{2,3},{3,0},{4,5},{5,6},{6,7},{7,4},{8,9},{9,10},{10,1... | collective-permute-start | bytes 393224 | tf_op jit(solution)/shard_map/ppermute | solution.py:14
  448.9 13.7 %collective-permute-start.11 = (bf16[16,32,1,128]{3,2,1,0:T(2,128)(2,1)S(1)}, bf16[16,32,1,128]{3,2,1,0:T(2,128)(2,1)S(1)}, u32[]{:S(2)}, u32[]{:S(2)}) collective-permute-start(bf16[16,32,1,128]{3,2,1,0:T(2,128)(2,1)S(1)} %copy-done.8), channel_id=1, source_target_pairs={{1,0},{2,1},{3,2},{0,3},{5,4},{6,5},{7,6},{4,7},{9,8},{10,9},{11,1... | collective-permute-start | bytes 393224 | tf_op jit(solution)/shard_map/ppermute | solution.py:16
  462.6 37.9 %copy-start.1 = (bf16[256,128]{1,0:T(8,128)(2,1)S(1)}, bf16[256,128]{1,0:T(8,128)(2,1)}, u32[]{:S(2)}) copy-start(bf16[256,128]{1,0:T(8,128)(2,1)} %param.33) | copy-start | bytes 196612
  (14 other events, 57.2 us)
Sparse Core Ops, SparseCore 0:
  366.8 127.5 all-reduce.1
where the time goes:
time: 508 us; the launch traced here: 507 us
  other arithmetic  254 us (50%)
  local copies, waits for them, and re-layouts  161 us (32%)
  matrix products  31.1 us (6%)
  waiting for transfers between devices  29.3 us (6%)
  starting transfers between devices  16.5 us (3%)
  between operations  15.3 us (3%)
    scatter-add x1, other arithmetic, on_device(): jax.ops.segment_sum(d_receiver, receiver_ids, cell_count, indices_are_sor...  76.2 us
    scatter-add x1, other arithmetic, on_device(): jax.ops.segment_sum(edge_new.astype(jnp.float32), receiver_ids, cell_coun...  76 us
    scatter-add x1, other arithmetic, on_device(): jax.ops.segment_sum(d_sender, sender_ids, flat_pad.shape[0])  66.6 us
    gather x1, local copies, waits for them, and re-layouts, on_device(): sender_rows = jnp.take(flat_pad, sender_ids, axis=0)  43.7 us
    gather x1, local copies, waits for them, and re-layouts, on_device(): receiver_rows = jnp.take(own_rows, receiver_ids, axis=0)  43.6 us
    gather x1, local copies, waits for them, and re-layouts, on_device(): jnp.take(dx_node[:, latent:], receiver_ids, axis=0)  41.5 us
    psum x1, waiting for transfers between devices, reduce_flat(): return lax.psum(flat_grads, ('gx', 'gy', 'gz'))  16.5 us
    unnamed x60, local copies, waits for them, and re-layouts  13.5 us
  transfers between devices with their start and end apart: 13, of which 5 were waited for; matrix products, arithmetic and copies ran while one was open for 28% of the time, Pallas kernels for 0%

commit v1 on v0

v1 whole, which is shorter than its diff:
```python
import functools

import jax
import jax.numpy as jnp
from jax import lax
from jax.experimental import pallas as pl
from jax.experimental.pallas import tpu as pltpu
from jax.sharding import PartitionSpec as P

F32 = jnp.float32
BF16 = jnp.bfloat16
TILE = 256
WIN = 80
WIDE = 128
ROUND = 16


def dot(left, right):
    return jnp.dot(left, right, preferred_element_type=F32)


def dot_t(left, right):
    return lax.dot_general(left, right, (((0,), (0,)), ((), ())), preferred_element_type=F32)


def dot_nt(left, right):
    return lax.dot_general(left, right, (((1,), (1,)), ((), ())), preferred_element_type=F32)


def sigma_of(values):
    return 0.5 + 0.5 * jnp.tanh(0.5 * values)


def fold_rows(values):
    return jnp.sum(values.reshape(-1, 8, values.shape[-1]), axis=0)


def layer_kernel(
    dims,
    stride,
    base_ref, count_ref,
    node_ref, edge_ref, cot_ref, cotn_ref, key_ref,
    w1e_ref, b1e_ref, w2e_ref, b2e_ref, w1n_ref, b1n_ref, w2n_ref,
    fxp_ref, fxm_ref, fyp_ref, fym_ref, fzp_ref, fzm_ref,
    gnode_ref, gedge_ref, raw_ref,
    oxp_ref, oxm_ref, oyp_ref, oym_ref, ozp_ref, ozm_ref,
    tab_ref, s_ref, r_ref, tmp_ref, z_ref, agg_ref, dagg_ref, bias_ref, rawr_ref, *g_refs,
):
    sx, sy, sz = dims
    cells = sx * sy * sz
    plane = sy * sz
    lat = node_ref.shape[1]
    tiles = edge_ref.shape[0] // TILE
    h = lat
    slab = 256
    slabs = cells // slab

    w1s = w1e_ref[h:2 * h, :]
    w1r = w1e_ref[2 * h:, :]

    for k in range(slabs):
        rows = pl.ds(k * slab, slab)
        s_ref[rows, :] = dot(node_ref[rows, :], w1s)
        r_ref[rows, :] = dot(node_ref[rows, :], w1r) + b1e_ref[...]

    def publish(d):
        for k in range(slabs):
            rows = pl.ds(k * slab, slab)
            tab_ref[d, rows, :] = (tmp_ref[rows, :] + r_ref[rows, :]).astype(BF16)
        tab_ref[d, pl.ds(cells, WIDE), :] = jnp.zeros((WIDE, h), BF16)

    def shift_up(by):
        for k in range(slabs):
            n = min(slab, cells - by - k * slab)
            if n > 0:
                tmp_ref[pl.ds(k * slab, n), :] = s_ref[pl.ds(k * slab + by, n), :]

    def shift_down(by):
        for k in range(slabs):
            n = min(slab, cells - by - k * slab)
            if n > 0:
                tmp_ref[pl.ds(k * slab + by, n), :] = s_ref[pl.ds(k * slab, n), :]

    shift_up(plane)
    tmp_ref[pl.ds(cells - plane, plane), :] = dot(fxp_ref[...], w1s)
    publish(0)
    shift_down(plane)
    tmp_ref[pl.ds(0, plane), :] = dot(fxm_ref[...], w1s)
    publish(1)
    shift_up(sz)
    face = dot(fyp_ref[...], w1s)
    for i in range(sx):
        tmp_ref[pl.ds(i * plane + plane - sz, sz), :] = face[i * sz:(i + 1) * sz]
    publish(2)
    shift_down(sz)
    face = dot(fym_ref[...], w1s)
    for i in range(sx):
        tmp_ref[pl.ds(i * plane, sz), :] = face[i * sz:(i + 1) * sz]
    publish(3)
    shift_up(1)
    tmp_ref[pl.ds(sz - 1, sx * sy, stride=sz), :] = dot(fzp_ref[...], w1s)
    publish(4)
    shift_down(1)
    tmp_ref[pl.ds(0, sx * sy, stride=sz), :] = dot(fzm_ref[...], w1s)
    publish(5)

    for k in range(slabs):
        rows = pl.ds(k * slab, slab)
        agg_ref[rows, :] = jnp.zeros((slab, h), F32)
        for g_ref in g_refs:
            g_ref[rows, :] = jnp.zeros((slab, h), F32)
    agg_ref[pl.ds(cells, WIDE), :] = jnp.zeros((WIDE, h), F32)
    dagg_ref[pl.ds(cells, WIDE), :] = jnp.zeros((WIDE, h), BF16)
    for g_ref in g_refs:
        g_ref[pl.ds(cells, WIDE), :] = jnp.zeros((WIDE, h), F32)
    rawr_ref[...] = jnp.zeros_like(rawr_ref)
    bias_ref[...] = jnp.zeros_like(bias_ref)

    lane_chunks = (6 * WIN + 127) // 128

    def lane_values():
        out = []
        for q in range(lane_chunks):
            m = lax.broadcasted_iota(jnp.int32, (1, 128), 1) + 128 * q
            d = jnp.zeros((1, 128), jnp.int32)
            for k in range(1, 6):
                d = d + (m >= k * WIN).astype(jnp.int32)
            out.append(jnp.where(m < 6 * WIN, m + d * (stride - WIN), -(1 << 30)))
        return out

    def columns(row):
        parts = [
            jnp.broadcast_to(row[:, q * 128:(q + 1) * 128], (128, 128)).T
            for q in range(TILE // 128)
        ]
        return jnp.concatenate(parts, axis=0)

    def hot_cols(col, b):
        col = col - b
        pieces = [jnp.where(col == v, 1.0, 0.0).astype(BF16) for v in lane_values()]
        return jnp.concatenate(pieces, axis=1)

    def gather_table(col, b):
        pieces = [tab_ref[d, pl.ds(b, WIN), :] for d in range(6)]
        pad = lane_chunks * 128 - 6 * WIN
        if pad:
            pieces.append(jnp.zeros((pad, h), BF16))
        return dot(hot_cols(col, b), jnp.concatenate(pieces, axis=0))

    def hot_cell_rows(row, b, width):
        cell = (row & (stride - 1)) - b
        return jnp.where(
            lax.broadcasted_iota(jnp.int32, (width, TILE), 0) == cell, 1.0, 0.0
        ).astype(BF16)

    def hot_cell_cols(col, b, width):
        cell = (col & (stride - 1)) - b
        return jnp.where(
            lax.broadcasted_iota(jnp.int32, (TILE, width), 1) == cell, 1.0, 0.0
        ).astype(BF16)

    def hot_dir_rows(row, b):
        iota = lax.broadcasted_iota(jnp.int32, (WIN, TILE), 0)
        pieces = [
            jnp.where(iota == row - (b + d * stride), 1.0, 0.0).astype(BF16) for d in range(6)
        ]
        return jnp.concatenate(pieces, axis=0)

    w1a = w1e_ref[:h, :]

    def forward_tile(t, slow):
        rows = pl.ds(pl.multiple_of(t * TILE, TILE), TILE)
        b = pl.multiple_of(base_ref[t], ROUND)
        row = key_ref[pl.ds(t, 1), :]
        col = columns(row)
        e = edge_ref[rows, :]
        z = dot(e, w1a) + gather_table(col, b)
        z_ref[rows, :] = z
        if slow:
            @pl.loop(1, count_ref[t])
            def _(w):
                z_ref[rows, :] += gather_table(col, pl.multiple_of(b + w * WIN, ROUND))
            z = z_ref[rows, :]
        u = (z * sigma_of(z)).astype(BF16)
        fresh = (e.astype(F32) + dot(u, w2e_ref[...]) + b2e_ref[...]).astype(BF16)

        def scatter(at):
            agg_ref[pl.ds(at, WIN), :] += dot(hot_cell_rows(row, at, WIN), fresh)

        scatter(b)
        if slow:
            @pl.loop(1, count_ref[t])
            def _(w):
                scatter(pl.multiple_of(b + w * WIN, ROUND))

    def backward_tile(t, slow):
        rows = pl.ds(pl.multiple_of(t * TILE, TILE), TILE)
        b = pl.multiple_of(base_ref[t], ROUND)
        row = key_ref[pl.ds(t, 1), :]
        col = columns(row)

        def gather(at):
            hot = hot_cell_cols(col, at, WIDE)
            if slow:
                keep = lax.broadcasted_iota(jnp.int32, (1, WIDE), 1) < WIN
                hot = jnp.where(keep, hot.astype(F32), 0.0).astype(BF16)
            return dot(hot, dagg_ref[pl.ds(at, WIDE), :])

        back = gather(b)
        if slow:
            def more(w, back):
                return back + gather(pl.multiple_of(b + w * WIN, ROUND))
            back = lax.fori_loop(1, count_ref[t], more, back)
        e = edge_ref[rows, :]
        d = (cot_ref[rows, :].astype(F32) + back).astype(BF16)
        z = z_ref[rows, :]
        s = sigma_of(z)
        u = z * s
        slope = s * (1.0 + z * (1.0 - s))
        dz = dot_nt(d, w2e_ref[...]) * slope
        dzb = dz.astype(BF16)
        gedge_ref[rows, :] = (d.astype(F32) + dot_nt(dzb, w1a)).astype(BF16)

        def scatter(at):
            out = dot(hot_dir_rows(row, at), dzb)
            for k, g_ref in enumerate(g_refs):
                g_ref[pl.ds(at, WIN), :] += out[k * WIN:(k + 1) * WIN]

        scatter(b)
        if slow:
            @pl.loop(1, count_ref[t])
            def _(w):
                scatter(pl.multiple_of(b + w * WIN, ROUND))
        raw_ref[0:h, :] += dot_t(e, dzb)
        raw_ref[3 * h:4 * h, :] += dot_t(u.astype(BF16), d)
        bias_ref[0] += fold_rows(dzb.astype(F32))
        bias_ref[1] += fold_rows(d.astype(F32))

    raw_ref[...] = jnp.zeros_like(raw_ref)
    most = lax.fori_loop(0, tiles, lambda t, m: jnp.maximum(m, count_ref[t]), 1)

    @pl.when(most == 1)
    def _():
        @pl.loop(0, tiles)
        def _(t):
            forward_tile(t, False)

    @pl.when(most > 1)
    def _():
        @pl.loop(0, tiles)
        def _(t):
            forward_tile(t, True)

    at = 4 * h

    @pl.loop(0, slabs)
    def _(k):
        rows = pl.ds(pl.multiple_of(k * slab, slab), slab)
        own = node_ref[rows, :]
        agg = agg_ref[rows, :].astype(BF16)
        cot = cotn_ref[rows, :]
        z = dot(own, w1n_ref[:h, :]) + dot(agg, w1n_ref[h:, :]) + b1n_ref[...]
        s = sigma_of(z)
        u = (z * s).astype(BF16)
        dz = (dot_nt(cot, w2n_ref[...]) * (s * (1.0 + z * (1.0 - s)))).astype(BF16)
        gnode_ref[rows, :] = cot.astype(F32) + dot_nt(dz, w1n_ref[:h, :])
        dagg_ref[rows, :] = dot_nt(dz, w1n_ref[h:, :]).astype(BF16)
        raw_ref[at:at + h, :] += dot_t(own, dz)
        raw_ref[at + h:at + 2 * h, :] += dot_t(agg, dz)
        raw_ref[at + 2 * h:at + 3 * h, :] += dot_t(u, cot)
        bias_ref[2] += fold_rows(dz.astype(F32))
        bias_ref[3] += fold_rows(cot.astype(F32))

    @pl.when(most == 1)
    def _():
        @pl.loop(0, tiles)
        def _(t):
            backward_tile(t, False)

    @pl.when(most > 1)
    def _():
        @pl.loop(0, tiles)
        def _(t):
            backward_tile(t, True)

    g0, g1, g2, g3, g4, g5 = g_refs
    for k in range(slabs):
        rows = pl.ds(k * slab, slab)
        total = g0[rows, :] + g1[rows, :] + g2[rows, :] + g3[rows, :] + g4[rows, :] + g5[rows, :]
        total = total.astype(BF16)
        gnode_ref[rows, :] += dot_nt(total, w1r)
        rawr_ref[...] += dot_t(node_ref[rows, :], total)
    raw_ref[2 * h:3 * h, :] = rawr_ref[...]

    acc = jnp.zeros((h, h), F32)

    def out_face(values, own_ref, out_ref):
        values = values.astype(BF16)
        out_ref[...] = dot_nt(values, w1s).astype(BF16)
        return dot_t(own_ref[...], values)

    acc += out_face(g0[pl.ds(cells - plane, plane), :], fxp_ref, oxp_ref)
    acc += out_face(g1[pl.ds(0, plane), :], fxm_ref, oxm_ref)
    pieces = [g2[pl.ds(i * plane + plane - sz, sz), :] for i in range(sx)]
    acc += out_face(jnp.concatenate(pieces, axis=0), fyp_ref, oyp_ref)
    pieces = [g3[pl.ds(i * plane, sz), :] for i in range(sx)]
    acc += out_face(jnp.concatenate(pieces, axis=0), fym_ref, oym_ref)
    acc += out_face(g4[pl.ds(sz - 1, sx * sy, stride=sz), :], fzp_ref, ozp_ref)
    acc += out_face(g5[pl.ds(0, sx * sy, stride=sz), :], fzm_ref, ozm_ref)
    for i in range(sx):
        g2[pl.ds(i * plane + plane - sz, sz), :] = jnp.zeros((sz, h), F32)
        g3[pl.ds(i * plane, sz), :] = jnp.zeros((sz, h), F32)
    g4[pl.ds(sz - 1, sx * sy, stride=sz), :] = jnp.zeros((sx * sy, h), F32)
    g5[pl.ds(0, sx * sy, stride=sz), :] = jnp.zeros((sx * sy, h), F32)

    tmp_ref[...] = jnp.zeros_like(tmp_ref)
    for g_ref, by in ((g0, plane), (g2, sz), (g4, 1)):
        for k in range(slabs):
            n = min(slab, cells - by - k * slab)
            if n > 0:
                tmp_ref[pl.ds(k * slab + by, n), :] += g_ref[pl.ds(k * slab, n), :]
    for g_ref, by in ((g1, plane), (g3, sz), (g5, 1)):
        for k in range(slabs):
            n = min(slab, cells - by - k * slab)
            if n > 0:
                tmp_ref[pl.ds(k * slab, n), :] += g_ref[pl.ds(k * slab + by, n), :]
    rawr_ref[...] = acc
    for k in range(slabs):
        rows = pl.ds(k * slab, slab)
        total = tmp_ref[rows, :].astype(BF16)
        gnode_ref[rows, :] += dot_nt(total, w1s)
        rawr_ref[...] += dot_t(node_ref[rows, :], total)
    raw_ref[h:2 * h, :] = rawr_ref[...]
    for k in range(4):
        raw_ref[7 * h + k:7 * h + k + 1, :] = jnp.sum(bias_ref[k], axis=0, keepdims=True)


def exchange(head, tail, axis):
    count = lax.axis_size(axis)
    up = [(i, (i + 1) % count) for i in range(count)]
    down = [((i + 1) % count, i) for i in range(count)]
    return lax.ppermute(head, axis, down), lax.ppermute(tail, axis, up)


def on_device(
    node_latent, edge_latent, senders, receivers,
    w1_edge, b1_edge, w2_edge, b2_edge, w1_node, b1_node, w2_node,
    cot_node, cot_edge,
):
    sx, sy, sz, lat = node_latent.shape
    cells = sx * sy * sz
    edges = edge_latent.shape[3]
    own = node_latent.reshape(cells, lat)
    faces = []
    faces += exchange(node_latent[0].reshape(-1, lat), node_latent[-1].reshape(-1, lat), "gx")
    faces += exchange(node_latent[:, 0].reshape(-1, lat), node_latent[:, -1].reshape(-1, lat), "gy")
    faces += exchange(
        node_latent[:, :, 0].reshape(-1, lat), node_latent[:, :, -1].reshape(-1, lat), "gz"
    )
    r = receivers.reshape(edges)
    s = senders.reshape(edges)
    padded = ((r // (sy * sz) + 1) * (sy + 2) + r // sz % sy + 1) * (sz + 2) + r % sz + 1
    diff = s - padded
    step_x = (sy + 2) * (sz + 2)
    step_y = sz + 2
    direction = jnp.where(
        diff == step_x, 0,
        jnp.where(
            diff == -step_x, 1,
            jnp.where(
                diff == step_y, 2, jnp.where(diff == -step_y, 3, jnp.where(diff == 1, 4, 5))
            ),
        ),
    )
    stride = 1
    while stride < cells + WIDE:
        stride *= 2
    tiles = edges // TILE
    keys = (direction * stride + r).reshape(tiles, TILE)
    grouped = r.reshape(tiles, TILE)
    base = grouped[:, 0] // ROUND * ROUND
    counts = (grouped[:, -1] - base) // WIN + 1

    face_rows = [f.shape[0] for f in faces]
    raw_rows = 7 * lat + 8
    vmem = pl.BlockSpec(memory_space=pltpu.VMEM)
    smem = pl.BlockSpec(memory_space=pltpu.SMEM)
    outs = pl.pallas_call(
        functools.partial(layer_kernel, (sx, sy, sz), stride),
        out_shape=[
            jax.ShapeDtypeStruct((cells, lat), F32),
            jax.ShapeDtypeStruct((edges, lat), BF16),
            jax.ShapeDtypeStruct((raw_rows, lat), F32),
        ] + [jax.ShapeDtypeStruct((n, lat), BF16) for n in face_rows],
        in_specs=[smem] * 2 + [vmem] * 18,
        out_specs=[vmem] * 9,
        scratch_shapes=[
            pltpu.VMEM((6, cells + WIDE, lat), BF16),
            pltpu.VMEM((cells, lat), F32),
            pltpu.VMEM((cells, lat), F32),
            pltpu.VMEM((cells, lat), F32),
            pltpu.VMEM((edges, lat), F32),
            pltpu.VMEM((cells + WIDE, lat), F32),
            pltpu.VMEM((cells + WIDE, lat), BF16),
            pltpu.VMEM((4, 8, lat), F32),
            pltpu.VMEM((lat, lat), F32),
        ] + [pltpu.VMEM((cells + WIDE, lat), F32)] * 6,
        compiler_params=pltpu.CompilerParams(vmem_limit_bytes=60 * 1024 * 1024),
        cost_estimate=pl.CostEstimate(
            flops=40 * edges * lat * lat, bytes_accessed=6 * edges * lat, transcendentals=0
        ),
    )(
        base, counts,
        own, edge_latent.reshape(edges, lat), cot_edge.reshape(edges, lat),
        cot_node.reshape(cells, lat), keys,
        w1_edge, b1_edge.reshape(1, lat), w2_edge, b2_edge.reshape(1, lat),
        w1_node, b1_node.reshape(1, lat), w2_node,
        *faces,
    )
    gnode, gedge, raw = outs[:3]
    oxp, oxm, oyp, oym, ozp, ozm = outs[3:]
    xm, xp = exchange(oxm, oxp, "gx")
    ym, yp = exchange(oym, oyp, "gy")
    zm, zp = exchange(ozm, ozp, "gz")
    grid = gnode.reshape(sx, sy, sz, lat)
    grid = grid.at[0].add(xp.reshape(sy, sz, lat).astype(F32))
    grid = grid.at[-1].add(xm.reshape(sy, sz, lat).astype(F32))
    grid = grid.at[:, 0].add(yp.reshape(sx, sz, lat).astype(F32))
    grid = grid.at[:, -1].add(ym.reshape(sx, sz, lat).astype(F32))
    grid = grid.at[:, :, 0].add(zp.reshape(sx, sy, lat).astype(F32))
    grid = grid.at[:, :, -1].add(zm.reshape(sx, sy, lat).astype(F32))
    grad_node = grid.astype(BF16)

    summed = lax.psum(raw, ("gx", "gy", "gz"))
    params = 7 * lat * lat + 4 * lat
    squares = jnp.sum(summed * summed)
    factor = 1.0 / jnp.maximum(1.0, jnp.sqrt(squares / params))
    scaled = summed * factor
    return (
        grad_node,
        gedge.reshape(edge_latent.shape),
        scaled[:3 * lat],
        scaled[3 * lat:4 * lat],
        scaled[4 * lat:6 * lat],
        scaled[6 * lat:7 * lat],
        scaled[7 * lat:7 * lat + 4],
    )


def solution(mesh):
    cell = P("gx", "gy", "gz", None)
    edge = P("gx", "gy", "gz", None, None)
    return jax.shard_map(
        on_device,
        mesh=mesh,
        in_specs=(cell, edge, cell, cell, P(), P(), P(), P(), P(), P(), P(), cell, edge),
        out_specs=(cell, edge, P(), P(), P(), P(), P()),
        check_vma=False,
    )
```

time: 508 us -> 241 us (0.47)
  other arithmetic: 254 us -> 17.7 us
  local copies, waits for them, and re-layouts: 161 us -> 23.1 us
  waiting for transfers between devices: 29.3 us -> 101 us
  Pallas kernels: 0 us -> 67 us
  matrix products: 31.1 us -> 0 us
    scatter-add x7 -> x3, other arithmetic: 219 us -> 4.24 us  [the longest x1 1.48 us: on_device(): grid = grid.at[-1].add(xm.reshape(sy, sz, lat).astype(F32))]
    gather x3 -> x0, local copies, waits for them, and re-layouts: 129 us -> none  [the longest x1 43.7 us: on_device(): sender_rows = jnp.take(flat_pad, sender_ids, axis=0)]
    psum x1, waiting for transfers between devices: 16.5 us -> 98.8 us  [on_device(): summed = lax.psum(raw, ('gx', 'gy', 'gz'))]
    pallas_call x0 -> x1, Pallas kernels: none -> 67 us  [on_device(): pl.pallas_call(functools.partial(layer_kernel, (sx, sy, sz), stride), out...]
    dot_general x13 -> x0, matrix products: 31.1 us -> none  [the longest x4 10.3 us: transposed_dot(): lax.dot_general(left, right, (((0,), (0,)), ((), ())), preferred_element_...]
    unnamed x60 -> x15, local copies, waits for them, and re-layouts: 13.5 us -> 1.22 us
    select_n x3 -> x0, other arithmetic: 10.9 us -> none  [the longest x2 10.1 us: on_device(): sender_rows = jnp.take(flat_pad, sender_ids, axis=0)]
    ppermute x12, waiting for transfers between devices: 12.8 us -> 2.68 us  [exchange(): return (lax.ppermute(head, axis, down), lax.ppermute(tail, axis, up))]
  transfers between devices with their start and end apart: 13 -> 13, of which waited for: 5 -> 2; matrix products, arithmetic and copies ran while one was open for 28% -> 14% of each run, Pallas kernels for 0% -> 0%
where the time goes in v1:
time: 241 us; the launch traced here: 240 us
  waiting for transfers between devices  101 us (42%)
  Pallas kernels  67 us (28%)
  local copies, waits for them, and re-layouts  23.1 us (10%)
  other arithmetic  17.7 us (7%)
  starting transfers between devices  15.8 us (7%)
  between operations  15 us (6%)
    psum x1, waiting for transfers between devices, on_device(): summed = lax.psum(raw, ('gx', 'gy', 'gz'))  98.8 us
    pallas_call x1, Pallas kernels, on_device(): pl.pallas_call(functools.partial(layer_kernel, (sx, sy, sz), stride), out...  67 us
    ppermute x12, starting transfers between devices, exchange(): return (lax.ppermute(head, axis, down), lax.ppermute(tail, axis, up))  15.8 us
    scatter-add x1, local copies, waits for them, and re-layouts, on_device(): grid = grid.at[:, :, 0].add(zp.reshape(sx, sy, lat).astype(F32))  7.54 us
    scatter-add x1, local copies, waits for them, and re-layouts, on_device(): grid = grid.at[:, :, -1].add(zm.reshape(sx, sy, lat).astype(F32))  7.54 us
  transfers between devices with their start and end apart: 13, of which 2 were waited for; matrix products, arithmetic and copies ran while one was open for 14% of the time, Pallas kernels for 0%

profile of v1, /device:TPU:0, one launch (start us, length us, event | category | flops | bytes accessed | tf_op | source)
XLA Modules:
  0.0 240.1 jit_solution(16603129913990703749)
XLA Ops:
  7.2 1.9 fusion.18
  9.1 5.1 %collective-permute-start.4 = (bf16[512,128]{1,0:T(8,128)(2,1)S(1)}, bf16[512,128]{1,0:T(8,128)(2,1)S(1)}, u32[]{:S(2)}, u32[]{:S(2)}) collective-permute-start(bf16[512,128]{1,0:T(8,128)(2,1)S(1)} %bitcast.39), channel_id=1, source_target_pairs={{1,0},{2,1},{3,2},{0,3},{5,4},{6,5},{7,6},{4,7},{9,8},{10,9},{11,1... | collective-permute-start | bytes 393224 | tf_op jit(solution)/shard_map/ppermute | solution.py:342
  14.3 0.8 fusion.20
  15.9 0.7 fusion.19
  16.6 1.6 collective-permute-start.2
  18.7 1.6 reduce.22
  20.3 1.6 reduce.23
  24.0 2.7 %collective-permute-done.3.fym_ref = bf16[64,128]{1,0:T(8,128)(2,1)S(1)} collective-permute-done((bf16[64,128]{1,0:T(8,128)(2,1)S(1)}, bf16[64,128]{1,0:T(8,128)(2,1)S(1)}, u32[]{:S(2)}, u32[]{:S(2)}) %collective-permute-start.3) | collective-permute-done | bytes 16416 | tf_op jit(solution)/shard_map/ppermute | solution.py:342
  27.4 67.0 %shard_map.180 = (f32[2048,128]{1,0:T(8,128)}, bf16[12288,128]{1,0:T(8,128)(2,1)}, f32[904,128]{1,0:T(8,128)}, bf16[128,128]{1,0:T(8,128)(2,1)}, bf16[128,128]{1...) custom-call(s32[48]{0:T(128)} %get-tuple-element.100.base_ref, ...), custom_call_target="tpu_custom_call" | custom-call | flops 8053063680 | bytes 9437184 | tf_op jit(solution)/shard_map/pallas_call | solution.py:388
  94.4 1.7 collective-permute-start.7
  96.7 1.5 collective-permute-start.9
  98.2 3.9 %collective-permute-start.11 = (bf16[512,128]{1,0:T(8,128)(2,1)}, bf16[512,128]{1,0:T(8,128)(2,1)S(1)}, u32[]{:S(2)}, u32[]{:S(2)}) collective-permute-start(bf16[512,128]{1,0:T(8,128)(2,1)} %get-tuple-element.94), channel_id=1, source_target_pairs={{1,0},{2,1},{3,2},{0,3},{5,4},{6,5},{7,6},{4,7},{9,8},{10,9},{11,1... | collective-permute-start | bytes 393224 | tf_op jit(solution)/shard_map/ppermute | solution.py:342
  102.1 0.8 convert_add_fusion
  103.6 1.5 fusion
  105.1 1.4 fusion.14
  106.4 1.4 fusion.13
  107.9 1.5 slice_add_fusion.1
  109.4 7.5 %scatter-add.26 = f32[16,32,4,128]{3,2,1,0:T(4,128)} dynamic-update-slice(f32[16,32,4,128]{3,2,1,0:T(4,128)} %fusion.13, f32[16,32,1,128]{3,2,1,0:T(1,128)S(1)} %slice_add_fusion.1, s32[]{:T(128)} %constant.232.clone.1, s32[]{:T(128)} %constant.232.clone.1, s32[]{:T(128)} %constant.232.clone.1, s32[]{:T(128)} %constant.232.clone.1) | dynamic-update-slice | bytes 524292 | tf_op jit(solution)/shard_map/scatter-add | solution.py:430
  116.9 1.6 slice_add_fusion
  118.6 7.5 %scatter-add.29 = f32[16,32,4,128]{3,2,1,0:T(4,128)} dynamic-update-slice(f32[16,32,4,128]{3,2,1,0:T(4,128)} %scatter-add.26, f32[16,32,1,128]{3,2,1,0:T(1,128)S(1)} %slice_add_fusion, s32[]{:T(128)} %constant.232.clone.1, s32[]{:T(128)} %constant.232.clone.1, s32[]{:T(128)} %constant.241.clone.1, s32[]{:T(128)} %constant.232.clone.1) | dynamic-update-slice | bytes 524292 | tf_op jit(solution)/shard_map/scatter-add | solution.py:431
  126.1 2.2 convert_element_type.78
  128.4 98.8 %all-reduce.2.cloned.1.call-done = f32[904,128]{1,0:T(8,128)} async-done(((f32[904,128]{1,0:T(8,128)}), f32[904,128]{1,0:T(8,128)}) %all-reduce.2.cloned.1.call-update) | async-done | bytes 462864 | tf_op jit(solution)/shard_map/psum | solution.py:434
  227.2 1.7 multiply_reduce_fusion
  229.6 1.1 broadcast_multiply_fusion
  (47 shorter events, 8.0 us)
Async XLA Ops:
  7.2 220.0 %all-reduce.2.cloned.1.call-start = ((), (), s32[]{:S(2)}) async-start(), calls=%async_computation | async-start | bytes 925696 | tf_op jit(solution)/shard_map/psum | solution.py:434
  9.1 17.5 %collective-permute-start.4 = (bf16[512,128]{1,0:T(8,128)(2,1)S(1)}, bf16[512,128]{1,0:T(8,128)(2,1)S(1)}, u32[]{:S(2)}, u32[]{:S(2)}) collective-permute-start(bf16[512,128]{1,0:T(8,128)(2,1)S(1)} %bitcast.39), channel_id=1, source_target_pairs={{1,0},{2,1},{3,2},{0,3},{5,4},{6,5},{7,6},{4,7},{9,8},{10,9},{11,1... | collective-permute-start | bytes 393224 | tf_op jit(solution)/shard_map/ppermute | solution.py:342
  14.3 12.4 %collective-permute-start.5 = (bf16[512,128]{1,0:T(8,128)(2,1)S(1)}, bf16[512,128]{1,0:T(8,128)(2,1)S(1)}, u32[]{:S(2)}, u32[]{:S(2)}) collective-permute-start(bf16[512,128]{1,0:T(8,128)(2,1)S(1)} %bitcast.40), channel_id=1, source_target_pairs={{0,1},{1,2},{2,3},{3,0},{4,5},{5,6},{6,7},{7,4},{8,9},{9,10},{10,1... | collective-permute-start | bytes 393224 | tf_op jit(solution)/shard_map/ppermute | solution.py:342
  15.1 11.5 %collective-permute-start = (bf16[128,128]{1,0:T(8,128)(2,1)S(1)}, bf16[128,128]{1,0:T(8,128)(2,1)S(1)}, u32[]{:S(2)}, u32[]{:S(2)}) collective-permute-start(bf16[128,128]{1,0:T(8,128)(2,1)S(1)} %bitcast.45), channel_id=1, source_target_pairs={{8,0},{16,8},{24,16},{0,24},{9,1},{17,9},{25,17},{1,25},{10,2},{18... | collective-permute-start | bytes 98312 | tf_op jit(solution)/shard_map/ppermute | solution.py:342
  15.9 10.8 %collective-permute-start.1 = (bf16[128,128]{1,0:T(8,128)(2,1)S(1)}, bf16[128,128]{1,0:T(8,128)(2,1)S(1)}, u32[]{:S(2)}, u32[]{:S(2)}) collective-permute-start(bf16[128,128]{1,0:T(8,128)(2,1)S(1)} %bitcast.44), channel_id=1, source_target_pairs={{0,8},{8,16},{16,24},{24,0},{1,9},{9,17},{17,25},{25,1},{2,10},{10... | collective-permute-start | bytes 98312 | tf_op jit(solution)/shard_map/ppermute | solution.py:342
  16.6 6.2 %collective-permute-start.2 = (bf16[64,128]{1,0:T(8,128)(2,1)S(1)}, bf16[64,128]{1,0:T(8,128)(2,1)S(1)}, u32[]{:S(2)}, u32[]{:S(2)}) collective-permute-start(bf16[64,128]{1,0:T(8,128)(2,1)S(1)} %bitcast.49), channel_id=1, source_target_pairs={{4,0},{0,4},{5,1},{1,5},{6,2},{2,6},{7,3},{3,7},{12,8},{8,12},{13,... | collective-permute-start | bytes 49160 | tf_op jit(solution)/shard_map/ppermute | solution.py:342
  22.8 3.9 %copy-start.4 = (bf16[64,128]{1,0:T(8,128)(2,1)}, bf16[64,128]{1,0:T(8,128)(2,1)S(1)}, u32[]{:S(2)}) copy-start(bf16[64,128]{1,0:T(8,128)(2,1)S(1)} %collective-permute-done.2.fyp_ref) | copy-start | bytes 49156
  22.8 3.8 %collective-permute-start.3 = (bf16[64,128]{1,0:T(8,128)(2,1)S(1)}, bf16[64,128]{1,0:T(8,128)(2,1)S(1)}, u32[]{:S(2)}, u32[]{:S(2)}) collective-permute-start(bf16[64,128]{1,0:T(8,128)(2,1)S(1)} %bitcast.48), channel_id=1, source_target_pairs={{0,4},{4,0},{1,5},{5,1},{2,6},{6,2},{3,7},{7,3},{8,12},{12,8},{9,1... | collective-permute-start | bytes 49160 | tf_op jit(solution)/shard_map/ppermute | solution.py:342
  26.6 0.6 copy-start.5
  26.6 0.6 copy-start.2
  26.6 0.6 copy-start.3
  26.6 0.7 copy-start
  26.7 0.7 copy-start.1
  94.4 3.9 %collective-permute-start.6 = (bf16[128,128]{1,0:T(8,128)(2,1)}, bf16[128,128]{1,0:T(8,128)(2,1)S(1)}, u32[]{:S(2)}, u32[]{:S(2)}) collective-permute-start(bf16[128,128]{1,0:T(8,128)(2,1)} %get-tuple-element.89), channel_id=1, source_target_pairs={{0,8},{8,16},{16,24},{24,0},{1,9},{9,17},{17,25},{25,1},{2,10},{10... | collective-permute-start | bytes 98312 | tf_op jit(solution)/shard_map/ppermute | solution.py:342
  94.4 9.2 %collective-permute-start.7 = (bf16[128,128]{1,0:T(8,128)(2,1)}, bf16[128,128]{1,0:T(8,128)(2,1)S(1)}, u32[]{:S(2)}, u32[]{:S(2)}) collective-permute-start(bf16[128,128]{1,0:T(8,128)(2,1)} %get-tuple-element.90), channel_id=1, source_target_pairs={{8,0},{16,8},{24,16},{0,24},{9,1},{17,9},{25,17},{1,25},{10,2},{18... | collective-permute-start | bytes 98312 | tf_op jit(solution)/shard_map/ppermute | solution.py:342
  96.2 8.9 %collective-permute-start.8 = (bf16[64,128]{1,0:T(8,128)(2,1)}, bf16[64,128]{1,0:T(8,128)(2,1)S(1)}, u32[]{:S(2)}, u32[]{:S(2)}) collective-permute-start(bf16[64,128]{1,0:T(8,128)(2,1)} %get-tuple-element.91), channel_id=1, source_target_pairs={{0,4},{4,0},{1,5},{5,1},{2,6},{6,2},{3,7},{7,3},{8,12},{12,8},{9,1... | collective-permute-start | bytes 49160 | tf_op jit(solution)/shard_map/ppermute | solution.py:342
  96.7 9.8 %collective-permute-start.9 = (bf16[64,128]{1,0:T(8,128)(2,1)}, bf16[64,128]{1,0:T(8,128)(2,1)S(1)}, u32[]{:S(2)}, u32[]{:S(2)}) collective-permute-start(bf16[64,128]{1,0:T(8,128)(2,1)} %get-tuple-element.92), channel_id=1, source_target_pairs={{4,0},{0,4},{5,1},{1,5},{6,2},{2,6},{7,3},{3,7},{12,8},{8,12},{13,... | collective-permute-start | bytes 49160 | tf_op jit(solution)/shard_map/ppermute | solution.py:342
  98.2 9.6 %collective-permute-start.10 = (bf16[512,128]{1,0:T(8,128)(2,1)}, bf16[512,128]{1,0:T(8,128)(2,1)S(1)}, u32[]{:S(2)}, u32[]{:S(2)}) collective-permute-start(bf16[512,128]{1,0:T(8,128)(2,1)} %get-tuple-element.93), channel_id=1, source_target_pairs={{0,1},{1,2},{2,3},{3,0},{4,5},{5,6},{6,7},{7,4},{8,9},{9,10},{10,1... | collective-permute-start | bytes 393224 | tf_op jit(solution)/shard_map/ppermute | solution.py:342
  98.2 18.7 %collective-permute-start.11 = (bf16[512,128]{1,0:T(8,128)(2,1)}, bf16[512,128]{1,0:T(8,128)(2,1)S(1)}, u32[]{:S(2)}, u32[]{:S(2)}) collective-permute-start(bf16[512,128]{1,0:T(8,128)(2,1)} %get-tuple-element.94), channel_id=1, source_target_pairs={{1,0},{2,1},{3,2},{0,3},{5,4},{6,5},{7,6},{4,7},{9,8},{10,9},{11,1... | collective-permute-start | bytes 393224 | tf_op jit(solution)/shard_map/ppermute | solution.py:342
Sparse Core Ops, SparseCore 0:
  98.3 128.7 all-reduce.1

commit v2 on v1

--- a/solution.py
+++ b/solution.py
@@ -42,9 +42,9 @@
     node_ref, edge_ref, cot_ref, cotn_ref, key_ref,
     w1e_ref, b1e_ref, w2e_ref, b2e_ref, w1n_ref, b1n_ref, w2n_ref,
     fxp_ref, fxm_ref, fyp_ref, fym_ref, fzp_ref, fzm_ref,
-    gnode_ref, gedge_ref, raw_ref,
+    gnode_ref, gedge_ref, rawb_ref,
     oxp_ref, oxm_ref, oyp_ref, oym_ref, ozp_ref, ozm_ref,
-    tab_ref, s_ref, r_ref, tmp_ref, z_ref, agg_ref, dagg_ref, bias_ref, rawr_ref, *g_refs,
+    tab_ref, s_ref, r_ref, tmp_ref, z_ref, agg_ref, dagg_ref, bias_ref, rawr_ref, raw_ref, *g_refs,
 ):
     sx, sy, sz = dims
     cells = sx * sy * sz
@@ -333,13 +333,177 @@
     raw_ref[h:2 * h, :] = rawr_ref[...]
     for k in range(4):
         raw_ref[7 * h + k:7 * h + k + 1, :] = jnp.sum(bias_ref[k], axis=0, keepdims=True)
-
-
-def exchange(head, tail, axis):
-    count = lax.axis_size(axis)
-    up = [(i, (i + 1) % count) for i in range(count)]
-    down = [((i + 1) % count, i) for i in range(count)]
-    return lax.ppermute(head, axis, down), lax.ppermute(tail, axis, up)
+    rawb_ref[...] = raw_ref[...].astype(BF16)
+
+
+MESH = pl.DeviceIdType.MESH
+AXES = ("gx", "gy", "gz")
+
+
+def neighbours():
+    here = [lax.axis_index(a) for a in AXES]
+    out = []
+    for k, a in enumerate(AXES):
+        count = lax.axis_size(a)
+        for step in (1, count - 1):
+            at = list(here)
+            at[k] = lax.rem(here[k] + step, count)
+            out.append(tuple(at))
+    return out
+
+
+def halo_kernel(dims, node_ref, *refs):
+    outs, sends, lands, tmp_ref, send_sem, recv_sem = (
+        refs[:6], refs[6:12], refs[12:18], refs[18], refs[19], refs[20]
+    )
+    sx, sy, sz = dims
+    plane = sy * sz
+    cells = sx * plane
+    ids = neighbours()
+    barrier = pltpu.get_barrier_semaphore()
+    for who in ids:
+        pl.semaphore_signal(barrier, inc=1, device_id=who, device_id_type=MESH)
+    for k in range(cells // 256):
+        rows = pl.ds(k * 256, 256)
+        tmp_ref[rows, :] = node_ref[rows, :].astype(F32)
+    sends[4][...] = tmp_ref[pl.ds(sz - 1, sx * sy, stride=sz), :].astype(BF16)
+    sends[5][...] = tmp_ref[pl.ds(0, sx * sy, stride=sz), :].astype(BF16)
+    sends[0][...] = node_ref[pl.ds(cells - plane, plane), :]
+    sends[1][...] = node_ref[pl.ds(0, plane), :]
+    sends[2][...] = jnp.concatenate(
+        [tmp_ref[pl.ds(i * plane + plane - sz, sz), :] for i in range(sx)], axis=0
+    ).astype(BF16)
+    sends[3][...] = jnp.concatenate(
+        [tmp_ref[pl.ds(i * plane, sz), :] for i in range(sx)], axis=0
+    ).astype(BF16)
+    pl.semaphore_wait(barrier, 6)
+    copies = []
+    for d in (4, 5, 0, 1, 2, 3):
+        copy = pltpu.make_async_remote_copy(
+            src_ref=sends[d], dst_ref=lands[d ^ 1],
+            send_sem=send_sem.at[d], recv_sem=recv_sem.at[d ^ 1],
+            device_id=ids[d], device_id_type=MESH,
+        )
+        copy.start()
+        copies.append((d, copy))
+    for d, copy in copies:
+        copy.wait_send()
+    for d, copy in copies:
+        copy.wait_recv()
+        outs[d ^ 1][...] = lands[d ^ 1][...]
+
+
+def reduce_kernel(dims, raw_ref, gnode_ref, *refs):
+    faces = refs[:6]
+    gout_ref, w1e_ref, w2e_ref, w1n_ref, w2n_ref, bias_ref = refs[6:12]
+    part_ref, sum_ref, all_ref, tmp_ref = refs[12:16]
+    lands = refs[16:22]
+    rs_send, rs_recv, ag_send, ag_recv, halo_send, halo_recv = refs[22:28]
+    sx, sy, sz = dims
+    plane = sy * sz
+    cells = sx * plane
+    h = gnode_ref.shape[1]
+    nx, ny, nz = [lax.axis_size(a) for a in AXES]
+    n = nx * ny * nz
+    ix, iy, iz = [lax.axis_index(a) for a in AXES]
+    me = (ix * ny + iy) * nz + iz
+
+    def rank(k):
+        return lax.rem(me + k, n)
+
+    def device(p):
+        return (p // (ny * nz), p // nz % ny, p % nz)
+
+    barrier = pltpu.get_barrier_semaphore()
+
+    @pl.loop(1, n)
+    def _(k):
+        pl.semaphore_signal(barrier, inc=1, device_id=device(rank(k)), device_id_type=MESH)
+
+    for k in range(cells // 256):
+        rows = pl.ds(k * 256, 256)
+        tmp_ref[rows, :] = gnode_ref[rows, :]
+    pl.semaphore_wait(barrier, n - 1)
+
+    def scatter(k):
+        p = rank(k)
+        return pltpu.make_async_remote_copy(
+            src_ref=raw_ref.at[p], dst_ref=part_ref.at[k],
+            send_sem=rs_send.at[k], recv_sem=rs_recv.at[k],
+            device_id=device(p), device_id_type=MESH,
+        )
+
+    def spread(k):
+        p = rank(k)
+        return pltpu.make_async_remote_copy(
+            src_ref=sum_ref, dst_ref=all_ref.at[me],
+            send_sem=ag_send.at[k], recv_sem=ag_recv.at[k],
+            device_id=device(p), device_id_type=MESH,
+        )
+
+    @pl.loop(1, n)
+    def _(k):
+        scatter(k).start()
+
+    ids = neighbours()
+    halos = []
+    for d in range(6):
+        halos.append(pltpu.make_async_remote_copy(
+            src_ref=faces[d], dst_ref=lands[d],
+            send_sem=halo_send.at[d], recv_sem=halo_recv.at[d],
+            device_id=ids[d], device_id_type=MESH,
+        ))
+        halos[-1].start()
+
+    @pl.loop(1, n)
+    def _(k):
+        scatter(k).wait_recv()
+
+    def add(k, total):
+        return total + part_ref[k].astype(F32)
+
+    total = lax.fori_loop(1, n, add, raw_ref[me].astype(F32)).astype(BF16)
+    sum_ref[...] = total
+    all_ref[me] = total
+
+    @pl.loop(1, n)
+    def _(k):
+        spread(k).start()
+
+    for d in range(6):
+        halos[d].wait_recv()
+    tmp_ref[pl.ds(0, plane), :] += lands[0][...].astype(F32)
+    tmp_ref[pl.ds(cells - plane, plane), :] += lands[1][...].astype(F32)
+    low, high = lands[2][...].astype(F32), lands[3][...].astype(F32)
+    for i in range(sx):
+        tmp_ref[pl.ds(i * plane, sz), :] += low[i * sz:(i + 1) * sz]
+        tmp_ref[pl.ds(i * plane + plane - sz, sz), :] += high[i * sz:(i + 1) * sz]
+    tmp_ref[pl.ds(0, sx * sy, stride=sz), :] += lands[4][...].astype(F32)
+    tmp_ref[pl.ds(sz - 1, sx * sy, stride=sz), :] += lands[5][...].astype(F32)
+    for k in range(cells // 256):
+        rows = pl.ds(k * 256, 256)
+        gout_ref[rows, :] = tmp_ref[rows, :].astype(BF16)
+
+    @pl.loop(1, n)
+    def _(k):
+        spread(k).wait_recv()
+
+    full = all_ref[...].astype(F32).reshape(-1, h)
+    squares = jnp.sum(jnp.sum(fold_rows(full * full), axis=0, keepdims=True), axis=1, keepdims=True)
+    factor = 1.0 / jnp.maximum(1.0, jnp.sqrt(squares / (7 * h * h + 4 * h)))
+    at = 0
+    for ref in (w1e_ref, w2e_ref, w1n_ref, w2n_ref, bias_ref):
+        rows = ref.shape[0]
+        ref[...] = full[at:at + rows] * factor
+        at += rows
+
+    @pl.loop(1, n)
+    def _(k):
+        scatter(k).wait_send()
+        spread(k).wait_send()
+
+    for d in range(6):
+        halos[d].wait_send()
 
 
 def on_device(
@@ -351,12 +515,23 @@
     cells = sx * sy * sz
     edges = edge_latent.shape[3]
     own = node_latent.reshape(cells, lat)
-    faces = []
-    faces += exchange(node_latent[0].reshape(-1, lat), node_latent[-1].reshape(-1, lat), "gx")
-    faces += exchange(node_latent[:, 0].reshape(-1, lat), node_latent[:, -1].reshape(-1, lat), "gy")
-    faces += exchange(
-        node_latent[:, :, 0].reshape(-1, lat), node_latent[:, :, -1].reshape(-1, lat), "gz"
-    )
+    vmem = pl.BlockSpec(memory_space=pltpu.VMEM)
+    smem = pl.BlockSpec(memory_space=pltpu.SMEM)
+    face_rows = [sy * sz, sy * sz, sx * sz, sx * sz, sx * sy, sx * sy]
+    dims = (sx, sy, sz)
+    faces = pl.pallas_call(
+        functools.partial(halo_kernel, dims),
+        out_shape=[jax.ShapeDtypeStruct((n, lat), BF16) for n in face_rows],
+        in_specs=[vmem],
+        out_specs=[vmem] * 6,
+        scratch_shapes=[pltpu.VMEM((n, lat), BF16) for n in face_rows] * 2
+        + [
+            pltpu.VMEM((cells, lat), F32),
+            pltpu.SemaphoreType.DMA((6,)),
+            pltpu.SemaphoreType.DMA((6,)),
+        ],
+        compiler_params=pltpu.CompilerParams(collective_id=0, has_side_effects=True),
+    )(own)
     r = receivers.reshape(edges)
     s = senders.reshape(edges)
     padded = ((r // (sy * sz) + 1) * (sy + 2) + r // sz % sy + 1) * (sz + 2) + r % sz + 1
@@ -381,16 +556,16 @@
     base = grouped[:, 0] // ROUND * ROUND
     counts = (grouped[:, -1] - base) // WIN + 1
 
-    face_rows = [f.shape[0] for f in faces]
-    raw_rows = 7 * lat + 8
-    vmem = pl.BlockSpec(memory_space=pltpu.VMEM)
-    smem = pl.BlockSpec(memory_space=pltpu.SMEM)
+    devices = 1
+    for axis in AXES:
+        devices *= lax.axis_size(axis)
+    chunk = -(-(7 * lat + 4) // (16 * devices)) * 16
     outs = pl.pallas_call(
-        functools.partial(layer_kernel, (sx, sy, sz), stride),
+        functools.partial(layer_kernel, dims, stride),
         out_shape=[
             jax.ShapeDtypeStruct((cells, lat), F32),
             jax.ShapeDtypeStruct((edges, lat), BF16),
-            jax.ShapeDtypeStruct((raw_rows, lat), F32),
+            jax.ShapeDtypeStruct((devices * chunk, lat), BF16),
         ] + [jax.ShapeDtypeStruct((n, lat), BF16) for n in face_rows],
         in_specs=[smem] * 2 + [vmem] * 18,
         out_specs=[vmem] * 9,
@@ -404,6 +579,7 @@
             pltpu.VMEM((cells + WIDE, lat), BF16),
             pltpu.VMEM((4, 8, lat), F32),
             pltpu.VMEM((lat, lat), F32),
+            pltpu.VMEM((devices * chunk, lat), F32),
         ] + [pltpu.VMEM((cells + WIDE, lat), F32)] * 6,
         compiler_params=pltpu.CompilerParams(vmem_limit_bytes=60 * 1024 * 1024),
         cost_estimate=pl.CostEstimate(
@@ -418,32 +594,33 @@
         *faces,
     )
     gnode, gedge, raw = outs[:3]
-    oxp, oxm, oyp, oym, ozp, ozm = outs[3:]
-    xm, xp = exchange(oxm, oxp, "gx")
-    ym, yp = exchange(oym, oyp, "gy")
-    zm, zp = exchange(ozm, ozp, "gz")
-    grid = gnode.reshape(sx, sy, sz, lat)
-    grid = grid.at[0].add(xp.reshape(sy, sz, lat).astype(F32))
-    grid = grid.at[-1].add(xm.reshape(sy, sz, lat).astype(F32))
-    grid = grid.at[:, 0].add(yp.reshape(sx, sz, lat).astype(F32))
-    grid = grid.at[:, -1].add(ym.reshape(sx, sz, lat).astype(F32))
-    grid = grid.at[:, :, 0].add(zp.reshape(sx, sy, lat).astype(F32))
-    grid = grid.at[:, :, -1].add(zm.reshape(sx, sy, lat).astype(F32))
-    grad_node = grid.astype(BF16)
-
-    summed = lax.psum(raw, ("gx", "gy", "gz"))
-    params = 7 * lat * lat + 4 * lat
-    squares = jnp.sum(summed * summed)
-    factor = 1.0 / jnp.maximum(1.0, jnp.sqrt(squares / params))
-    scaled = summed * factor
+    out = pl.pallas_call(
+        functools.partial(reduce_kernel, dims),
+        out_shape=[
+            jax.ShapeDtypeStruct((cells, lat), BF16),
+            jax.ShapeDtypeStruct((3 * lat, lat), F32),
+            jax.ShapeDtypeStruct((lat, lat), F32),
+            jax.ShapeDtypeStruct((2 * lat, lat), F32),
+            jax.ShapeDtypeStruct((lat, lat), F32),
+            jax.ShapeDtypeStruct((4, lat), F32),
+        ],
+        in_specs=[vmem] * 8,
+        out_specs=[vmem] * 6,
+        scratch_shapes=[
+            pltpu.VMEM((devices, chunk, lat), BF16),
+            pltpu.VMEM((chunk, lat), BF16),
+            pltpu.VMEM((devices, chunk, lat), BF16),
+            pltpu.VMEM((cells, lat), F32),
+        ]
+        + [pltpu.VMEM((n, lat), BF16) for n in face_rows]
+        + [pltpu.SemaphoreType.DMA((devices,))] * 4
+        + [pltpu.SemaphoreType.DMA((6,))] * 2,
+        compiler_params=pltpu.CompilerParams(collective_id=1, has_side_effects=True),
+    )(raw.reshape(devices, chunk, lat), gnode, *outs[3:])
     return (
-        grad_node,
+        out[0].reshape(node_latent.shape),
         gedge.reshape(edge_latent.shape),
-        scaled[:3 * lat],
-        scaled[3 * lat:4 * lat],
-        scaled[4 * lat:6 * lat],
-        scaled[6 * lat:7 * lat],
-        scaled[7 * lat:7 * lat + 4],
+        *out[1:],
     )
 
 

time: 241 us -> 124 us (0.51)
  waiting for transfers between devices: 101 us -> 0 us
  Pallas kernels: 67 us -> 108 us
  starting transfers between devices: 15.8 us -> 0 us
  between operations: 15 us -> 0.68 us
  other arithmetic: 17.7 us -> 4.41 us
  local copies, waits for them, and re-layouts: 23.1 us -> 10.1 us
    psum x1 -> x0, waiting for transfers between devices: 98.8 us -> none  [on_device(): summed = lax.psum(raw, ('gx', 'gy', 'gz'))]
    pallas_call x1 -> x3, Pallas kernels: 67 us -> 108 us  [the longest x1 67 us: on_device(): pl.pallas_call(functools.partial(layer_kernel, dims, stride), out_shape=[...]
    ppermute x12 -> x0, starting transfers between devices: 15.8 us -> none  [exchange(): return (lax.ppermute(head, axis, down), lax.ppermute(tail, axis, up))]
    scatter-add x3 -> x0, local copies, waits for them, and re-layouts: 15.7 us -> none  [the longest x1 7.54 us: on_device(): grid = grid.at[:, :, 0].add(zp.reshape(sx, sy, lat).astype(F32))]
    unnamed x15 -> x7, local copies, waits for them, and re-layouts: 1.22 us -> 9.94 us
    slice x7 -> x0, local copies, waits for them, and re-layouts: 6.01 us -> none  [the longest x1 1.87 us: on_device(): node_latent[:, :, -1].reshape(-1, lat)]
    scatter-add x3 -> x0, other arithmetic: 4.24 us -> none  [the longest x1 1.48 us: on_device(): grid = grid.at[-1].add(xm.reshape(sy, sz, lat).astype(F32))]
    add x3 -> x0, other arithmetic: 4 us -> none  [the longest x1 1.64 us: on_device(): grid = grid.at[:, :, -1].add(zm.reshape(sx, sy, lat).astype(F32))]
  transfers between devices with their start and end apart: 13 -> 0, of which waited for: 2 -> 0; matrix products, arithmetic and copies ran while one was open for 14% -> 0% of each run, Pallas kernels for 0% -> 0%
where the time goes in v2:
time: 124 us
  Pallas kernels  108 us (87%)
  local copies, waits for them, and re-layouts  10.1 us (8%)
  other arithmetic  4.41 us (4%)
    pallas_call x1, Pallas kernels, on_device(): pl.pallas_call(functools.partial(layer_kernel, dims, stride), out_shape=[...  67 us
    pallas_call x1, Pallas kernels, on_device(): pl.pallas_call(functools.partial(reduce_kernel, dims), out_shape=[jax.Sha...  28.3 us
    pallas_call x1, Pallas kernels, on_device(): pl.pallas_call(functools.partial(halo_kernel, dims), out_shape=[jax.Shape...  13.1 us
    unnamed x7, local copies, waits for them, and re-layouts  9.94 us
    unnamed x2, other arithmetic  3.12 us

profile of v2, /device:TPU:0, one launch (start us, length us, event | category | flops | bytes accessed | tf_op | source)
XLA Modules:
  0.0 123.6 jit_solution(14184808959503824027)
XLA Ops:
  0.6 0.5 broadcast.94
  1.1 1.6 %reduce.11 = s32[12288]{0:T(1024)S(1)} reduce(s32[1,1,1,12288]{3,2,1,0:T(1,128)} %param.15, s32[]{:T(128)} %broadcast.94), dimensions={0,1,2}, to_apply=%param.15.reduce_sub_computation.3 | reduce | bytes 98308 | tf_op args[2]
  2.7 1.6 %reduce.10 = s32[12288]{0:T(1024)S(1)} reduce(s32[1,1,1,12288]{3,2,1,0:T(1,128)} %param.16, s32[]{:T(128)} %broadcast.94), dimensions={0,1,2}, to_apply=%param.16.reduce_sub_computation.3 | reduce | bytes 98308 | tf_op args[3]
  4.3 0.7 multiply_add_fusion.key_ref
  5.1 0.2 slice_reduce_fusion
  5.2 0.5 fusion.12
  5.8 13.1 %shard_map.180 = (bf16[128,128]{1,0:T(8,128)(2,1)}, bf16[128,128]{1,0:T(8,128)(2,1)}, bf16[64,128]{1,0:T(8,128)(2,1)}, bf16[64,128]{1,0:T(8,128)(2,1)}, bf16[512...) custom-call(bf16[2048,128]{1,0:T(8,128)(2,1)} %bitcast.10), custom_call_target="tpu_custom_call" | custom-call | tf_op jit(solution)/shard_map/pallas_call | solution.py:522
  18.9 67.0 %shard_map.181 = (f32[2048,128]{1,0:T(8,128)}, bf16[12288,128]{1,0:T(8,128)(2,1)}, bf16[1024,128]{1,0:T(8,128)(2,1)}, bf16[128,128]{1,0:T(8,128)(2,1)}, bf16[128...) custom-call(s32[48]{0:T(128)} %get-tuple-element.52.base_ref, ...), custom_call_target="tpu_custom_call" | custom-call | flops 8053063680 | bytes 9437184 | tf_op jit(solution)/shard_map/pallas_call | solution.py:563
  85.9 28.3 %shard_map.182 = (bf16[2048,128]{1,0:T(8,128)(2,1)}, f32[384,128]{1,0:T(8,128)}, f32[128,128]{1,0:T(8,128)}, f32[256,128]{1,0:T(8,128)}, f32[128,128]{1,0:T(8,128)}, /*index=5*/f32[4,128]{1,0:T(4,128)}) custom-call(bf16[32,32,128]{2,1,0:T(8,128)(2,1)} %bitcast.13, f32[2048,128]{1,0:T(8,128)} %get-tuple-element.35.gnode_ref, ...), custom_call_target="tpu_custom_call" | custom-call | tf_op jit(solution)/shard_map/pallas_call | solution.py:597
  114.2 2.0 %copy.26 = bf16[16,32,4,128]{3,2,1,0:T(4,128)(2,1)} copy(bf16[16,32,4,128]{3,2,1,0:T(4,128)(2,1)} %bitcast.12) | data formatting | bytes 1048576
  116.2 1.6 %copy.27 = f32[384,128]{1,0:T(8,128)} copy(f32[384,128]{1,0:T(8,128)} %get-tuple-element.62) | data formatting | bytes 393216
  117.8 1.5 %copy.28 = f32[128,128]{1,0:T(8,128)} copy(f32[128,128]{1,0:T(8,128)} %get-tuple-element.63) | data formatting | bytes 131072
  119.3 1.6 %copy.29 = f32[256,128]{1,0:T(8,128)} copy(f32[256,128]{1,0:T(8,128)} %get-tuple-element.64) | data formatting | bytes 262144
  120.9 1.5 %copy.30 = f32[128,128]{1,0:T(8,128)} copy(f32[128,128]{1,0:T(8,128)} %get-tuple-element.65) | data formatting | bytes 131072
  122.3 1.3 %copy.31 = f32[4,128]{1,0:T(4,128)} copy(f32[4,128]{1,0:T(4,128)} %get-tuple-element.66) | data formatting | bytes 4096
  (2 shorter events, 0.0 us)

commit v3 on v2

--- a/solution.py
+++ b/solution.py
@@ -241,7 +241,7 @@
 
     @pl.when(most == 1)
     def _():
-        @pl.loop(0, tiles)
+        @pl.loop(0, tiles, unroll=2)
         def _(t):
             forward_tile(t, False)
 
@@ -273,7 +273,7 @@
 
     @pl.when(most == 1)
     def _():
-        @pl.loop(0, tiles)
+        @pl.loop(0, tiles, unroll=2)
         def _(t):
             backward_tile(t, False)
 
@@ -395,10 +395,10 @@
 
 def reduce_kernel(dims, raw_ref, gnode_ref, *refs):
     faces = refs[:6]
-    gout_ref, w1e_ref, w2e_ref, w1n_ref, w2n_ref, bias_ref = refs[6:12]
-    part_ref, sum_ref, all_ref, tmp_ref = refs[12:16]
-    lands = refs[16:22]
-    rs_send, rs_recv, ag_send, ag_recv, halo_send, halo_recv = refs[22:28]
+    gout_ref, allout_ref = refs[6:8]
+    part_ref, sum_ref, all_ref, tmp_ref = refs[8:12]
+    lands = refs[12:18]
+    rs_send, rs_recv, ag_send, ag_recv, halo_send, halo_recv = refs[18:24]
     sx, sy, sz = dims
     plane = sy * sz
     cells = sx * plane
@@ -488,6 +488,20 @@
     def _(k):
         spread(k).wait_recv()
 
+    allout_ref[...] = all_ref[...]
+
+    @pl.loop(1, n)
+    def _(k):
+        scatter(k).wait_send()
+        spread(k).wait_send()
+
+    for d in range(6):
+        halos[d].wait_send()
+
+
+def finish_kernel(all_ref, gin_ref, gout_ref, w1e_ref, w2e_ref, w1n_ref, w2n_ref, bias_ref):
+    h = gin_ref.shape[1]
+    gout_ref[...] = gin_ref[...]
     full = all_ref[...].astype(F32).reshape(-1, h)
     squares = jnp.sum(jnp.sum(fold_rows(full * full), axis=0, keepdims=True), axis=1, keepdims=True)
     factor = 1.0 / jnp.maximum(1.0, jnp.sqrt(squares / (7 * h * h + 4 * h)))
@@ -496,14 +510,6 @@
         rows = ref.shape[0]
         ref[...] = full[at:at + rows] * factor
         at += rows
-
-    @pl.loop(1, n)
-    def _(k):
-        scatter(k).wait_send()
-        spread(k).wait_send()
-
-    for d in range(6):
-        halos[d].wait_send()
 
 
 def on_device(
@@ -594,18 +600,14 @@
         *faces,
     )
     gnode, gedge, raw = outs[:3]
-    out = pl.pallas_call(
+    gsum, full = pl.pallas_call(
         functools.partial(reduce_kernel, dims),
         out_shape=[
             jax.ShapeDtypeStruct((cells, lat), BF16),
-            jax.ShapeDtypeStruct((3 * lat, lat), F32),
-            jax.ShapeDtypeStruct((lat, lat), F32),
-            jax.ShapeDtypeStruct((2 * lat, lat), F32),
-            jax.ShapeDtypeStruct((lat, lat), F32),
-            jax.ShapeDtypeStruct((4, lat), F32),
+            jax.ShapeDtypeStruct((devices, chunk, lat), BF16),
         ],
         in_specs=[vmem] * 8,
-        out_specs=[vmem] * 6,
+        out_specs=[vmem] * 2,
         scratch_shapes=[
             pltpu.VMEM((devices, chunk, lat), BF16),
             pltpu.VMEM((chunk, lat), BF16),
@@ -617,6 +619,19 @@
         + [pltpu.SemaphoreType.DMA((6,))] * 2,
         compiler_params=pltpu.CompilerParams(collective_id=1, has_side_effects=True),
     )(raw.reshape(devices, chunk, lat), gnode, *outs[3:])
+    out = pl.pallas_call(
+        finish_kernel,
+        out_shape=[
+            jax.ShapeDtypeStruct((cells, lat), BF16),
+            jax.ShapeDtypeStruct((3 * lat, lat), F32),
+            jax.ShapeDtypeStruct((lat, lat), F32),
+            jax.ShapeDtypeStruct((2 * lat, lat), F32),
+            jax.ShapeDtypeStruct((lat, lat), F32),
+            jax.ShapeDtypeStruct((4, lat), F32),
+        ],
+        in_specs=[vmem] * 2,
+        out_specs=[vmem] * 6,
+    )(full, gsum)
     return (
         out[0].reshape(node_latent.shape),
         gedge.reshape(edge_latent.shape),

time: 124 us -> 105 us (0.85)
  local copies, waits for them, and re-layouts: 10.1 us -> 0.72 us
  Pallas kernels: 108 us -> 99.3 us
    pallas_call x1, Pallas kernels: 67 us -> 56.1 us  [on_device(): pl.pallas_call(functools.partial(layer_kernel, dims, stride), out_shape=[...]
    unnamed x7 -> x1, local copies, waits for them, and re-layouts: 9.94 us -> 0.51 us
    pallas_call x0 -> x1, Pallas kernels: none -> 2.17 us  [on_device(): pl.pallas_call(finish_kernel, out_shape=[jax.ShapeDtypeStruct((cells, lat...]
where the time goes in v3:
time: 105 us
  Pallas kernels  99.3 us (95%)
  other arithmetic  4.41 us (4%)
    pallas_call x1, Pallas kernels, on_device(): pl.pallas_call(functools.partial(layer_kernel, dims, stride), out_shape=[...  56.1 us
    pallas_call x1, Pallas kernels, on_device(): pl.pallas_call(functools.partial(reduce_kernel, dims), out_shape=[jax.Sha...  28 us
    pallas_call x1, Pallas kernels, on_device(): pl.pallas_call(functools.partial(halo_kernel, dims), out_shape=[jax.Shape...  13.1 us
    unnamed x2, other arithmetic  3.12 us
    pallas_call x1, Pallas kernels, on_device(): pl.pallas_call(finish_kernel, out_shape=[jax.ShapeDtypeStruct((cells, lat...  2.17 us

profile of v3, /device:TPU:0, one launch (start us, length us, event | category | flops | bytes accessed | tf_op | source)
XLA Modules:
  0.0 105.1 jit_solution(5627925502528641045)
XLA Ops:
  0.6 0.5 broadcast.94
  1.1 1.6 %reduce.11 = s32[12288]{0:T(1024)S(1)} reduce(s32[1,1,1,12288]{3,2,1,0:T(1,128)} %param.15, s32[]{:T(128)} %broadcast.94), dimensions={0,1,2}, to_apply=%param.15.reduce_sub_computation.3 | reduce | bytes 98308 | tf_op args[2]
  2.7 1.6 %reduce.10 = s32[12288]{0:T(1024)S(1)} reduce(s32[1,1,1,12288]{3,2,1,0:T(1,128)} %param.16, s32[]{:T(128)} %broadcast.94), dimensions={0,1,2}, to_apply=%param.16.reduce_sub_computation.3 | reduce | bytes 98308 | tf_op args[3]
  4.3 0.7 multiply_add_fusion.key_ref
  5.1 0.2 slice_reduce_fusion
  5.2 0.5 fusion.12
  5.8 13.1 %shard_map.180 = (bf16[128,128]{1,0:T(8,128)(2,1)}, bf16[128,128]{1,0:T(8,128)(2,1)}, bf16[64,128]{1,0:T(8,128)(2,1)}, bf16[64,128]{1,0:T(8,128)(2,1)}, bf16[512...) custom-call(bf16[2048,128]{1,0:T(8,128)(2,1)} %bitcast.10), custom_call_target="tpu_custom_call" | custom-call | tf_op jit(solution)/shard_map/pallas_call | solution.py:528
  18.9 56.1 %shard_map.181 = (f32[2048,128]{1,0:T(8,128)}, bf16[12288,128]{1,0:T(8,128)(2,1)}, bf16[1024,128]{1,0:T(8,128)(2,1)}, bf16[128,128]{1,0:T(8,128)(2,1)}, bf16[128...) custom-call(s32[48]{0:T(128)} %get-tuple-element.56.base_ref, ...), custom_call_target="tpu_custom_call" | custom-call | flops 8053063680 | bytes 9437184 | tf_op jit(solution)/shard_map/pallas_call | solution.py:569
  75.0 28.0 %shard_map.182 = (bf16[2048,128]{1,0:T(8,128)(2,1)}, bf16[32,32,128]{2,1,0:T(8,128)(2,1)}) custom-call(bf16[32,32,128]{2,1,0:T(8,128)(2,1)} %bitcast.12, f32[2048,128]{1,0:T(8,128)} %get-tuple-element.37.gnode_ref, bf16[128,128]{1,0:T(8,128)(2,1)} %get-tuple-element.38.refs_0_, bf16[128,128]{1,0:T(8,128)(2,1)} %get-tuple-element.39.refs_1_, ...), custom_call_target="tpu_custom_call" | custom-call | tf_op jit(solution)/shard_map/pallas_call | solution.py:603
  103.0 2.2 %shard_map.183 = (bf16[2048,128]{1,0:T(8,128)(2,1)}, f32[384,128]{1,0:T(8,128)}, f32[128,128]{1,0:T(8,128)}, f32[256,128]{1,0:T(8,128)}, f32[128,128]{1,0:T(8,128)}, /*index=5*/f32[4,128]{1,0:T(4,128)}) custom-call(bf16[32,32,128]{2,1,0:T(8,128)(2,1)} %get-tuple-element.44.all_ref, bf16[2048,128]{1,0:T(8,128)(2,1)} %get-tuple-element.45.gin_ref), custom_call_target="tpu_custom_call" | custom-call | tf_op jit(solution)/shard_map/pallas_call | solution.py:622
  (2 shorter events, 0.0 us)

commit v4 on v3

--- a/solution.py
+++ b/solution.py
@@ -241,7 +241,7 @@
 
     @pl.when(most == 1)
     def _():
-        @pl.loop(0, tiles, unroll=2)
+        @pl.loop(0, tiles, unroll=4)
         def _(t):
             forward_tile(t, False)
 
@@ -273,7 +273,7 @@
 
     @pl.when(most == 1)
     def _():
-        @pl.loop(0, tiles, unroll=2)
+        @pl.loop(0, tiles, unroll=4)
         def _(t):
             backward_tile(t, False)
 

time: 105 us -> 100 us (0.952)
  Pallas kernels: 99.3 us -> 94.3 us
    pallas_call x1, Pallas kernels: 56.1 us -> 51.1 us  [on_device(): pl.pallas_call(functools.partial(layer_kernel, dims, stride), out_shape=[...]
where the time goes in v4:
time: 100 us
  Pallas kernels  94.3 us (94%)
  other arithmetic  4.41 us (4%)
    pallas_call x1, Pallas kernels, on_device(): pl.pallas_call(functools.partial(layer_kernel, dims, stride), out_shape=[...  51.1 us
    pallas_call x1, Pallas kernels, on_device(): pl.pallas_call(functools.partial(reduce_kernel, dims), out_shape=[jax.Sha...  28 us
    pallas_call x1, Pallas kernels, on_device(): pl.pallas_call(functools.partial(halo_kernel, dims), out_shape=[jax.Shape...  13.1 us
    unnamed x2, other arithmetic  3.12 us
    pallas_call x1, Pallas kernels, on_device(): pl.pallas_call(finish_kernel, out_shape=[jax.ShapeDtypeStruct((cells, lat...  2.17 us

profile of v4, /device:TPU:0, one launch (start us, length us, event | category | flops | bytes accessed | tf_op | source)
XLA Modules:
  0.0 100.1 jit_solution(17484224976454162459)
XLA Ops:
  0.6 0.5 broadcast.94
  1.1 1.6 %reduce.11 = s32[12288]{0:T(1024)S(1)} reduce(s32[1,1,1,12288]{3,2,1,0:T(1,128)} %param.15, s32[]{:T(128)} %broadcast.94), dimensions={0,1,2}, to_apply=%param.15.reduce_sub_computation.3 | reduce | bytes 98308 | tf_op args[2]
  2.7 1.6 %reduce.10 = s32[12288]{0:T(1024)S(1)} reduce(s32[1,1,1,12288]{3,2,1,0:T(1,128)} %param.16, s32[]{:T(128)} %broadcast.94), dimensions={0,1,2}, to_apply=%param.16.reduce_sub_computation.3 | reduce | bytes 98308 | tf_op args[3]
  4.3 0.7 multiply_add_fusion.key_ref
  5.1 0.2 slice_reduce_fusion
  5.2 0.5 fusion.12
  5.8 13.1 %shard_map.180 = (bf16[128,128]{1,0:T(8,128)(2,1)}, bf16[128,128]{1,0:T(8,128)(2,1)}, bf16[64,128]{1,0:T(8,128)(2,1)}, bf16[64,128]{1,0:T(8,128)(2,1)}, bf16[512...) custom-call(bf16[2048,128]{1,0:T(8,128)(2,1)} %bitcast.10), custom_call_target="tpu_custom_call" | custom-call | tf_op jit(solution)/shard_map/pallas_call | solution.py:528
  18.9 51.1 %shard_map.181 = (f32[2048,128]{1,0:T(8,128)}, bf16[12288,128]{1,0:T(8,128)(2,1)}, bf16[1024,128]{1,0:T(8,128)(2,1)}, bf16[128,128]{1,0:T(8,128)(2,1)}, bf16[128...) custom-call(s32[48]{0:T(128)} %get-tuple-element.56.base_ref, ...), custom_call_target="tpu_custom_call" | custom-call | flops 8053063680 | bytes 9437184 | tf_op jit(solution)/shard_map/pallas_call | solution.py:569
  69.9 28.0 %shard_map.182 = (bf16[2048,128]{1,0:T(8,128)(2,1)}, bf16[32,32,128]{2,1,0:T(8,128)(2,1)}) custom-call(bf16[32,32,128]{2,1,0:T(8,128)(2,1)} %bitcast.12, f32[2048,128]{1,0:T(8,128)} %get-tuple-element.37.gnode_ref, bf16[128,128]{1,0:T(8,128)(2,1)} %get-tuple-element.38.refs_0_, bf16[128,128]{1,0:T(8,128)(2,1)} %get-tuple-element.39.refs_1_, ...), custom_call_target="tpu_custom_call" | custom-call | tf_op jit(solution)/shard_map/pallas_call | solution.py:603
  97.9 2.2 %shard_map.183 = (bf16[2048,128]{1,0:T(8,128)(2,1)}, f32[384,128]{1,0:T(8,128)}, f32[128,128]{1,0:T(8,128)}, f32[256,128]{1,0:T(8,128)}, f32[128,128]{1,0:T(8,128)}, /*index=5*/f32[4,128]{1,0:T(4,128)}) custom-call(bf16[32,32,128]{2,1,0:T(8,128)(2,1)} %get-tuple-element.44.all_ref, bf16[2048,128]{1,0:T(8,128)(2,1)} %get-tuple-element.45.gin_ref), custom_call_target="tpu_custom_call" | custom-call | tf_op jit(solution)/shard_map/pallas_call | solution.py:622
  (2 shorter events, 0.0 us)
